TPU v7x, 128 devices: a whole 4x4x4 slice. The times are simulated.
128 devices in a mesh: pipe: 2 (over core), dp: 16 (over x, z), mp: 4 (over y).
Axes of the slice: x: 4, y: 4, z: 4, core: 2. Of those that a mesh axis runs over, the one named last changes fastest.
Arguments:
- hidden_states: bfloat16 [64, 64, 4096], P('dp'), may hold values from -6 to 6
- up_weight: bfloat16 [2, 4096, 7168], P('pipe', 'dp', 'mp'), may hold values from -0.09375 to 0.09375
- down_weight: bfloat16 [2, 7168, 4096], P('pipe', 'mp', 'dp'), may hold values from -0.0625 to 0.0625
- layer_gain: float32 [2, 4096], P('pipe'), may hold values from 0.5 to 1.5
- final_gain: float32 [4096], replicated, may hold values from 0.5 to 1.5
- unembedding: bfloat16 [32768, 4096], P(('pipe', 'mp')), may hold values from -32 to 32
- target_ids: int32 [64, 64], P('dp'), may hold values from 0 to 32767
- response_masks: int32 [64, 64], P('dp'), may hold values from 0 to 1, as said below
- anchor_logps: float32 [64, 64], P('dp'), may hold values from -14 to -10
- pairing: int32 [16, 4], P('dp'), may hold values from 0 to 3, each once within a row
Outputs:
- token_logps: float32 [64, 64], P('dp')
- seq_logps: float32 [64], P('dp')
- pair_losses: float32 [32], P('dp')
Inputs may be any that keep to these rules, and one draw needn't show every extreme that they name: response_masks is 1 on one unbroken run of at least one position per sequence, starting at or after position 8, and 0 elsewhere.
All inputs are finite; a program needn't handle non-finite values.
Results may differ from a plain program's by a relative error of at most 0.0075.
Values may be sent and summed in bfloat16 or wider, within the bound.
A program may use at most 192 MiB of HBM per device.

v0:
```python
import jax
import jax.numpy as jnp
from jax import lax
from jax.sharding import PartitionSpec as P

SEQ_MB = 1


epsilon = 1e-05
ipo_tau = 0.5


def copy_for_each(x, axis):
    copies = jnp.broadcast_to(x, (lax.axis_size(axis), *x.shape))
    return lax.all_to_all(copies, axis, split_axis=0, concat_axis=0, tiled=True)


def of_everyone(x, axis):
    everything = copy_for_each(x, axis)
    return jnp.sum(everything, axis=0)


def in_blocks(x, dim, peers):
    before, after = (x.shape[:dim], x.shape[dim + 1 :])
    return jnp.moveaxis(x.reshape(*before, peers, -1, *after), dim, 0)


def sent_and_summed(x, axis, dim):
    parts = in_blocks(x, dim, lax.axis_size(axis))
    arrived = lax.all_to_all(parts, axis, split_axis=0, concat_axis=0, tiled=True)
    return arrived.sum(axis=0)


def laid_out(parts, dim):
    parts = jnp.moveaxis(parts, 0, dim)
    lengths = parts.shape
    return parts.reshape(*lengths[:dim], lengths[dim] * lengths[dim + 1], *lengths[dim + 2 :])


def collect(x, axis, dim):
    parts = copy_for_each(x, axis)
    return laid_out(parts, dim)


def from_behind(value, axis, steps):
    count = lax.axis_size(axis)
    pairs = [(source, (source + steps) % count) for source in range(count)]
    return lax.ppermute(value, axis, pairs)


def packed_total(arrays, axis):
    vector, at, done = (jnp.concatenate([a.reshape(-1) for a in arrays]), 0, [])
    so_far = of_everyone(vector, axis)
    for a in arrays:
        done.append(so_far[at : at + a.size].reshape(a.shape))
        at += a.size
    return tuple(done)


def rms_scale(values, gain_row):
    mean_square = jnp.mean(values * values, axis=-1, keepdims=True)
    return values * lax.rsqrt(mean_square + epsilon) * gain_row


def shards(
    hidden_states,
    up_weight,
    down_weight,
    layer_gain,
    final_gain,
    unembedding,
    target_ids,
    response_masks,
    anchor_logps,
    pairing,
):
    seq_count, length, model_width = hidden_states.shape
    micro_count = seq_count // SEQ_MB
    batch_rows = SEQ_MB * length
    mask_values = response_masks.astype(jnp.float32)
    local_counts = jnp.sum(mask_values, axis=1)
    counts = of_everyone(local_counts, "dp")
    up_full, down_full = (
        lax.all_gather(up_weight, "dp", axis=1, tiled=True),
        lax.all_gather(down_weight, "dp", axis=2, tiled=True),
    )
    up_matrix = up_full[0]
    down_matrix = down_full[0]
    gain_row = layer_gain[0]
    section_index = lax.axis_index("pipe")

    def layer_partial(states):
        wide_states = states.astype(jnp.float32)
        normed = rms_scale(wide_states, gain_row).astype(jnp.bfloat16)
        active = jax.nn.silu(jnp.dot(normed, up_matrix, preferred_element_type=jnp.float32)).astype(
            jnp.bfloat16
        )
        return (wide_states, jnp.dot(active, down_matrix, preferred_element_type=jnp.float32))

    share_width = model_width // lax.axis_size("mp")
    column_start = lax.axis_index("mp") * share_width

    def run_layer(states):
        wide_states, partial_sum = layer_partial(states)
        summed = sent_and_summed(partial_sum, "mp", 1)
        residual_share = lax.dynamic_slice_in_dim(wide_states, column_start, share_width, 1)
        return (residual_share + summed).astype(jnp.bfloat16)

    def widen(rows):
        return collect(rows, "mp", 1)

    def advance(loop_state, step_index):
        incoming, finished = loop_state
        fresh_rows = lax.dynamic_index_in_dim(
            hidden_states, jnp.minimum(step_index, micro_count - 1), 0, keepdims=False
        )
        states = jnp.where(section_index == 0, fresh_rows, widen(incoming))
        output = run_layer(states)
        passed = from_behind(output, "pipe", 1)
        final_rows = jnp.where(section_index == 0, passed, output)
        slot_index = jnp.maximum(step_index - 1, 0)
        previous = lax.dynamic_index_in_dim(finished, slot_index, 0, keepdims=False)
        stored = jnp.where(step_index > 0, final_rows, previous)
        finished = lax.dynamic_update_index_in_dim(finished, stored, slot_index, 0)
        return ((passed, finished), None)

    start_state = (
        jnp.zeros((batch_rows, share_width), jnp.bfloat16),
        jnp.zeros((micro_count, batch_rows, share_width), jnp.bfloat16),
    )
    step_range = jnp.arange(micro_count + 1, dtype=jnp.int32)
    (unused_rows, finished), unused_out = lax.scan(advance, start_state, step_range)
    finals = widen(finished.reshape(seq_count * length, share_width))
    normed_final = rms_scale(finals.astype(jnp.float32), final_gain).astype(jnp.bfloat16)
    logits = lax.dot_general(
        normed_final, unembedding, (((1,), (1,)), ((), ())), preferred_element_type=jnp.float32
    )
    vocab_start = lax.axis_index(("pipe", "mp")) * unembedding.shape[0]
    local_ids = target_ids.reshape(-1) - vocab_start
    columns = lax.broadcasted_iota(jnp.int32, logits.shape, 1)
    picked = jnp.sum(jnp.where(columns == local_ids[:, None], logits, 0.0), axis=1)
    local_top = jnp.max(logits, axis=1)
    local_sum = jnp.sum(jnp.exp(logits - local_top[:, None]), axis=1)
    top_value = lax.pmax(local_top, ("pipe", "mp"))
    exp_total, picked_all = packed_total(
        (local_sum * jnp.exp(local_top - top_value), picked), ("pipe", "mp")
    )
    token_logps = (picked_all - top_value - jnp.log(exp_total)).reshape(seq_count, length)
    mean_length = counts / (lax.axis_size("dp") * SEQ_MB)
    divisor = jnp.repeat(mean_length, SEQ_MB)
    policy = jnp.sum(mask_values * token_logps, axis=1) / divisor
    anchor = jnp.sum(mask_values * anchor_logps, axis=1) / divisor
    log_gaps = policy - anchor
    positions = jnp.arange(seq_count, dtype=jnp.int32)
    chosen = jnp.sum(
        jnp.where(pairing[0, 0::2][:, None] == positions[None, :], log_gaps[None, :], 0.0), axis=1
    )
    rejected = jnp.sum(
        jnp.where(pairing[0, 1::2][:, None] == positions[None, :], log_gaps[None, :], 0.0), axis=1
    )
    losses = (chosen - rejected - 0.5 / ipo_tau) ** 2
    return (token_logps, policy, losses)


def solution(mesh):
    return jax.shard_map(
        shards,
        mesh=mesh,
        in_specs=(
            P("dp", None, None),
            P("pipe", "dp", "mp"),
            P("pipe", "mp", "dp"),
            P("pipe", None),
            P(),
            P(("pipe", "mp"), None),
            P("dp", None),
            P("dp", None),
            P("dp", None),
            P("dp", None),
        ),
        out_specs=(P("dp", None), P("dp"), P("dp")),
        check_vma=False,
    )
```

profile of v0, /device:TPU:1, one launch (start us, length us, event | category | flops | bytes accessed | tf_op | source)
XLA Modules:
  0.0 571.5 jit_solution(7204187557270797478)
XLA Ops:
  7.2 0.7 all-gather.5.cloned.1.call-update
  7.9 0.7 all-gather.3.cloned.1.call-update
  8.7 112.6 %all-gather.5.cloned.1.call-done = bf16[1,1792,4096]{2,1,0:T(8,128)(2,1)} async-done(((bf16[1,1792,256]{2,1,0:T(8,128)(2,1)}), bf16[1,1792,4096]{2,1,0:T(8,128)(2,1)}) %all-gather.5.cloned.1.call-update) | async-done | bytes 14680080 | tf_op jit(solution)/shard_map/all_gather | solution.py:85
  121.2 103.3 %all-gather.3.cloned.1.call-done = bf16[1,4096,1792]{2,1,0:T(8,128)(2,1)} async-done(((bf16[1,256,1792]{2,1,0:T(8,128)(2,1)}), bf16[1,4096,1792]{2,1,0:T(8,128)(2,1)}) %all-gather.3.cloned.1.call-update) | async-done | bytes 14680080 | tf_op jit(solution)/shard_map/all_gather | solution.py:84
  224.6 249.5 %while.14 = (s32[]{:T(128)}, bf16[64,1024]{1,0:T(8,128)(2,1)S(1)}, bf16[4,64,1024]{2,1,0:T(8,128)(2,1)S(1)}, pred[]{:T(512)}, s32[5]{0:T(128)S(1)}, /*index=5*/b...) while((s32[]{:T(128)}, bf16[64,1024]{1,0:T(8,128)(2,1)S(1)}, ...), condition=%wide.region_3.4_spmd, body=%wide.region_0.3_spmd.sunk | while | flops 1881915520 | bytes 44385648 | solution.py:132
  224.6 0.9 broadcast_in_dim.71
  225.5 4.0 all-to-all-start
  229.5 0.6 dynamic_slice.36
  230.7 7.0 %all-to-all-done = bf16[4,64,1024]{2,1,0:T(8,128)(2,1)S(1)} async-done(((bf16[4,64,1024]{2,1,0:T(8,128)(2,1)}), bf16[4,64,1024]{2,1,0:T(8,128)(2,1)S(1)}, u32[]{:S(2)}, u32[]{:S(2)}) %all-to-all-start) | async-done | bytes 524320 | tf_op jit(solution)/shard_map/while/body/eval_jaxpr/all_to_all | solution.py:15
  237.7 1.3 multiply_reduce_fusion.5
  239.1 14.9 %fusion.22 = f32[64,4096]{1,0:T(8,128)S(1)} fusion(bf16[1792,4096]{1,0:T(8,128)(2,1)} %get-tuple-element.276, bf16[4096,1792]{1,0:T(8,128)(2,1)} %get-tuple-element.275, f32[64,4096]{1,0:T(8,128)S(1)} %get-tuple-element.231, f32[4096]{0:T(1024)S(1)} %bitcast.75, f32[64]{0:T(128)S(1)} %add_rsqrt_fusion.3), kind=kOutput, calls=%fused_computation.9.clone.1 | convolution fusion | flops 1880408064 | bytes 31473920 | tf_op jit(solution)/shard_map/while/body/eval_jaxpr/dot_general | solution.py:98
  254.0 15.2 %all_to_all.36 = f32[4,64,1024]{2,1,0:T(8,128)S(1)} all-to-all(f32[4,64,1024]{2,1,0:T(8,128)S(1)} %bitcast.71), channel_id=1, replica_groups=mesh['pipe'=2,'dp'=16,'mp'=4] {'mp'}, dimensions={0} | all-to-all | bytes 2097152 | tf_op jit(solution)/shard_map/while/body/eval_jaxpr/all_to_all | solution.py:30
  269.3 3.4 collective-permute-start
  274.0 0.9 broadcast_in_dim.71
  274.9 3.5 all-to-all-start
  278.3 0.6 dynamic_slice.36
  279.5 8.2 %all-to-all-done = bf16[4,64,1024]{2,1,0:T(8,128)(2,1)S(1)} async-done(((bf16[4,64,1024]{2,1,0:T(8,128)(2,1)}), bf16[4,64,1024]{2,1,0:T(8,128)(2,1)S(1)}, u32[]{:S(2)}, u32[]{:S(2)}) %all-to-all-start) | async-done | bytes 524320 | tf_op jit(solution)/shard_map/while/body/eval_jaxpr/all_to_all | solution.py:15
  287.8 1.3 multiply_reduce_fusion.5
  289.1 14.9 %fusion.22 = f32[64,4096]{1,0:T(8,128)S(1)} fusion(bf16[1792,4096]{1,0:T(8,128)(2,1)} %get-tuple-element.276, bf16[4096,1792]{1,0:T(8,128)(2,1)} %get-tuple-element.275, f32[64,4096]{1,0:T(8,128)S(1)} %get-tuple-element.231, f32[4096]{0:T(1024)S(1)} %bitcast.75, f32[64]{0:T(128)S(1)} %add_rsqrt_fusion.3), kind=kOutput, calls=%fused_computation.9.clone.1 | convolution fusion | flops 1880408064 | bytes 31473920 | tf_op jit(solution)/shard_map/while/body/eval_jaxpr/dot_general | solution.py:98
  304.1 16.6 %all_to_all.36 = f32[4,64,1024]{2,1,0:T(8,128)S(1)} all-to-all(f32[4,64,1024]{2,1,0:T(8,128)S(1)} %bitcast.71), channel_id=1, replica_groups=mesh['pipe'=2,'dp'=16,'mp'=4] {'mp'}, dimensions={0} | all-to-all | bytes 2097152 | tf_op jit(solution)/shard_map/while/body/eval_jaxpr/all_to_all | solution.py:30
  320.8 1.9 collective-permute-start
  324.0 0.9 broadcast_in_dim.71
  324.9 3.5 all-to-all-start
  328.4 0.6 dynamic_slice.36
  329.5 8.2 %all-to-all-done = bf16[4,64,1024]{2,1,0:T(8,128)(2,1)S(1)} async-done(((bf16[4,64,1024]{2,1,0:T(8,128)(2,1)}), bf16[4,64,1024]{2,1,0:T(8,128)(2,1)S(1)}, u32[]{:S(2)}, u32[]{:S(2)}) %all-to-all-start) | async-done | bytes 524320 | tf_op jit(solution)/shard_map/while/body/eval_jaxpr/all_to_all | solution.py:15
  337.8 1.3 multiply_reduce_fusion.5
  339.1 14.9 %fusion.22 = f32[64,4096]{1,0:T(8,128)S(1)} fusion(bf16[1792,4096]{1,0:T(8,128)(2,1)} %get-tuple-element.276, bf16[4096,1792]{1,0:T(8,128)(2,1)} %get-tuple-element.275, f32[64,4096]{1,0:T(8,128)S(1)} %get-tuple-element.231, f32[4096]{0:T(1024)S(1)} %bitcast.75, f32[64]{0:T(128)S(1)} %add_rsqrt_fusion.3), kind=kOutput, calls=%fused_computation.9.clone.1 | convolution fusion | flops 1880408064 | bytes 31473920 | tf_op jit(solution)/shard_map/while/body/eval_jaxpr/dot_general | solution.py:98
  354.1 16.6 %all_to_all.36 = f32[4,64,1024]{2,1,0:T(8,128)S(1)} all-to-all(f32[4,64,1024]{2,1,0:T(8,128)S(1)} %bitcast.71), channel_id=1, replica_groups=mesh['pipe'=2,'dp'=16,'mp'=4] {'mp'}, dimensions={0} | all-to-all | bytes 2097152 | tf_op jit(solution)/shard_map/while/body/eval_jaxpr/all_to_all | solution.py:30
  370.8 1.9 collective-permute-start
  374.0 0.9 broadcast_in_dim.71
  374.9 3.5 all-to-all-start
  378.4 0.6 dynamic_slice.36
  379.6 8.2 %all-to-all-done = bf16[4,64,1024]{2,1,0:T(8,128)(2,1)S(1)} async-done(((bf16[4,64,1024]{2,1,0:T(8,128)(2,1)}), bf16[4,64,1024]{2,1,0:T(8,128)(2,1)S(1)}, u32[]{:S(2)}, u32[]{:S(2)}) %all-to-all-start) | async-done | bytes 524320 | tf_op jit(solution)/shard_map/while/body/eval_jaxpr/all_to_all | solution.py:15
  387.8 1.3 multiply_reduce_fusion.5
  389.2 14.9 %fusion.22 = f32[64,4096]{1,0:T(8,128)S(1)} fusion(bf16[1792,4096]{1,0:T(8,128)(2,1)} %get-tuple-element.276, bf16[4096,1792]{1,0:T(8,128)(2,1)} %get-tuple-element.275, f32[64,4096]{1,0:T(8,128)S(1)} %get-tuple-element.231, f32[4096]{0:T(1024)S(1)} %bitcast.75, f32[64]{0:T(128)S(1)} %add_rsqrt_fusion.3), kind=kOutput, calls=%fused_computation.9.clone.1 | convolution fusion | flops 1880408064 | bytes 31473920 | tf_op jit(solution)/shard_map/while/body/eval_jaxpr/dot_general | solution.py:98
  404.1 16.6 %all_to_all.36 = f32[4,64,1024]{2,1,0:T(8,128)S(1)} all-to-all(f32[4,64,1024]{2,1,0:T(8,128)S(1)} %bitcast.71), channel_id=1, replica_groups=mesh['pipe'=2,'dp'=16,'mp'=4] {'mp'}, dimensions={0} | all-to-all | bytes 2097152 | tf_op jit(solution)/shard_map/while/body/eval_jaxpr/all_to_all | solution.py:30
  420.9 1.9 collective-permute-start
  424.1 0.9 broadcast_in_dim.71
  425.0 3.5 all-to-all-start
  428.4 0.6 dynamic_slice.36
  429.6 8.2 %all-to-all-done = bf16[4,64,1024]{2,1,0:T(8,128)(2,1)S(1)} async-done(((bf16[4,64,1024]{2,1,0:T(8,128)(2,1)}), bf16[4,64,1024]{2,1,0:T(8,128)(2,1)S(1)}, u32[]{:S(2)}, u32[]{:S(2)}) %all-to-all-start) | async-done | bytes 524320 | tf_op jit(solution)/shard_map/while/body/eval_jaxpr/all_to_all | solution.py:15
  437.9 1.3 multiply_reduce_fusion.5
  439.2 14.9 %fusion.22 = f32[64,4096]{1,0:T(8,128)S(1)} fusion(bf16[1792,4096]{1,0:T(8,128)(2,1)} %get-tuple-element.276, bf16[4096,1792]{1,0:T(8,128)(2,1)} %get-tuple-element.275, f32[64,4096]{1,0:T(8,128)S(1)} %get-tuple-element.231, f32[4096]{0:T(1024)S(1)} %bitcast.75, f32[64]{0:T(128)S(1)} %add_rsqrt_fusion.3), kind=kOutput, calls=%fused_computation.9.clone.1 | convolution fusion | flops 1880408064 | bytes 31473920 | tf_op jit(solution)/shard_map/while/body/eval_jaxpr/dot_general | solution.py:98
  454.2 16.6 %all_to_all.36 = f32[4,64,1024]{2,1,0:T(8,128)S(1)} all-to-all(f32[4,64,1024]{2,1,0:T(8,128)S(1)} %bitcast.71), channel_id=1, replica_groups=mesh['pipe'=2,'dp'=16,'mp'=4] {'mp'}, dimensions={0} | all-to-all | bytes 2097152 | tf_op jit(solution)/shard_map/while/body/eval_jaxpr/all_to_all | solution.py:30
  470.9 1.9 collective-permute-start
  474.1 0.2 copy.24
  474.3 1.5 broadcast_in_dim.59
  475.8 3.6 all-to-all-start.2
  479.6 26.1 %all-to-all-done.2 = bf16[4,256,1024]{1,2,0:T(8,128)(2,1)S(1)} async-done(((bf16[4,256,1024]{1,2,0:T(8,128)(2,1)}), bf16[4,256,1024]{1,2,0:T(8,128)(2,1)S(1)}, u32[]{:S(2)}, u32[]{:S(2)}) %all-to-all-start.2) | async-done | bytes 2097184 | tf_op jit(solution)/shard_map/all_to_all | solution.py:15
  505.7 0.6 multiply_reduce_fusion.1
  506.3 1.7 fusion.8
  508.0 17.6 %fusion.12 = (f32[256]{0:T(256)S(1)}, f32[256,4096]{1,0:T(8,128)}) fusion(bf16[256,4096]{0,1:T(8,128)(2,1)} %fusion.8, bf16[4096,4096]{1,0:T(8,128)(2,1)} %param.17), kind=kOutput, calls=%fused_computation.39 | convolution fusion | flops 8590983168 | bytes 39846912 | tf_op jit(solution)/shard_map/dot_general | solution.py:135
  525.6 14.3 %pmax.7 = f32[256]{0:T(256)S(1)} all-reduce(f32[256]{0:T(256)S(1)} %get-tuple-element.166), channel_id=1, replica_groups=mesh['pipe'=2,'dp'=16,'mp'=4] {'pipe','mp'}, use_global_device_ids=true, to_apply=%region_7.8 | all-reduce | flops 256 | bytes 2048 | tf_op jit(solution)/shard_map/pmax | solution.py:144
  539.9 3.3 exponential_reduce_fusion
  543.3 7.8 %all_to_all.35 = f32[8,1,512]{2,1,0:T(1,128)S(1)} all-to-all(f32[8,1,512]{2,1,0:T(1,128)S(1)} %broadcast_in_dim.61), channel_id=1, replica_groups=mesh['pipe'=2,'dp'=16,'mp'=4] {'pipe','mp'}, dimensions={0} | all-to-all | bytes 32768 | tf_op jit(solution)/shard_map/all_to_all | solution.py:15
  551.2 0.1 multiply_reduce_fusion.2
  551.3 0.6 broadcast_in_dim.62
  551.9 5.0 all-to-all-start.4
  556.9 0.1 slice.14
  557.0 0.1 slice.15
  557.1 6.2 %all-to-all-done.4 = f32[16,1,4]{2,1,0:T(1,128)S(1)} async-done(((f32[16,1,4]{2,1,0:T(1,128)}), f32[16,1,4]{2,1,0:T(1,128)S(1)}, u32[]{:S(2)}, u32[]{:S(2)}) %all-to-all-start.4) | async-done | bytes 288 | tf_op jit(solution)/shard_map/all_to_all | solution.py:15
  563.4 0.5 divide_subtract_fusion
  563.9 0.2 fusion.10
  564.1 0.5 add_multiply_fusion
  (77 shorter events, 1.9 us)
Async XLA Ops:
  7.2 114.1 %all-gather.5.cloned.1.call-start = ((), (), s32[]{:S(2)}) async-start(), calls=%async_computation.6 | async-start | bytes 15597568 | tf_op jit(solution)/shard_map/all_gather | solution.py:85
  7.9 216.6 %all-gather.3.cloned.1.call-start = ((), (), s32[]{:S(2)}) async-start(), calls=%async_computation.5 | async-start | bytes 15597568 | tf_op jit(solution)/shard_map/all_gather | solution.py:84
  224.6 14.4 %copy-start = (f32[1,4096]{1,0:T(1,128)S(1)}, f32[1,4096]{1,0:T(1,128)}, u32[]{:S(2)}) copy-start(f32[1,4096]{1,0:T(1,128)} %get-tuple-element.274) | copy-start | bytes 49156 | tf_op jit(solution)/shard_map/while
  225.5 12.2 %all-to-all-start = ((bf16[4,64,1024]{2,1,0:T(8,128)(2,1)}), bf16[4,64,1024]{2,1,0:T(8,128)(2,1)S(1)}, u32[]{:S(2)}, u32[]{:S(2)}) async-start(bf16[4,64,1024]{2,1,0:T(8,128)(2,1)} %broadcast_in_dim.71), calls=%async_computation | async-start | bytes 1048576 | tf_op jit(solution)/shard_map/while/body/eval_jaxpr/all_to_all | solution.py:15
  269.3 4.5 collective-permute-start
  274.0 15.1 %copy-start = (f32[1,4096]{1,0:T(1,128)S(1)}, f32[1,4096]{1,0:T(1,128)}, u32[]{:S(2)}) copy-start(f32[1,4096]{1,0:T(1,128)} %get-tuple-element.274) | copy-start | bytes 49156 | tf_op jit(solution)/shard_map/while
  274.9 12.9 %all-to-all-start = ((bf16[4,64,1024]{2,1,0:T(8,128)(2,1)}), bf16[4,64,1024]{2,1,0:T(8,128)(2,1)S(1)}, u32[]{:S(2)}, u32[]{:S(2)}) async-start(bf16[4,64,1024]{2,1,0:T(8,128)(2,1)} %broadcast_in_dim.71), calls=%async_computation | async-start | bytes 1048576 | tf_op jit(solution)/shard_map/while/body/eval_jaxpr/all_to_all | solution.py:15
  320.8 3.1 collective-permute-start
  324.0 15.1 %copy-start = (f32[1,4096]{1,0:T(1,128)S(1)}, f32[1,4096]{1,0:T(1,128)}, u32[]{:S(2)}) copy-start(f32[1,4096]{1,0:T(1,128)} %get-tuple-element.274) | copy-start | bytes 49156 | tf_op jit(solution)/shard_map/while
  324.9 12.9 %all-to-all-start = ((bf16[4,64,1024]{2,1,0:T(8,128)(2,1)}), bf16[4,64,1024]{2,1,0:T(8,128)(2,1)S(1)}, u32[]{:S(2)}, u32[]{:S(2)}) async-start(bf16[4,64,1024]{2,1,0:T(8,128)(2,1)} %broadcast_in_dim.71), calls=%async_computation | async-start | bytes 1048576 | tf_op jit(solution)/shard_map/while/body/eval_jaxpr/all_to_all | solution.py:15
  370.8 3.1 collective-permute-start
  374.0 15.1 %copy-start = (f32[1,4096]{1,0:T(1,128)S(1)}, f32[1,4096]{1,0:T(1,128)}, u32[]{:S(2)}) copy-start(f32[1,4096]{1,0:T(1,128)} %get-tuple-element.274) | copy-start | bytes 49156 | tf_op jit(solution)/shard_map/while
  374.9 12.9 %all-to-all-start = ((bf16[4,64,1024]{2,1,0:T(8,128)(2,1)}), bf16[4,64,1024]{2,1,0:T(8,128)(2,1)S(1)}, u32[]{:S(2)}, u32[]{:S(2)}) async-start(bf16[4,64,1024]{2,1,0:T(8,128)(2,1)} %broadcast_in_dim.71), calls=%async_computation | async-start | bytes 1048576 | tf_op jit(solution)/shard_map/while/body/eval_jaxpr/all_to_all | solution.py:15
  420.9 3.1 collective-permute-start
  424.1 15.1 %copy-start = (f32[1,4096]{1,0:T(1,128)S(1)}, f32[1,4096]{1,0:T(1,128)}, u32[]{:S(2)}) copy-start(f32[1,4096]{1,0:T(1,128)} %get-tuple-element.274) | copy-start | bytes 49156 | tf_op jit(solution)/shard_map/while
  425.0 12.9 %all-to-all-start = ((bf16[4,64,1024]{2,1,0:T(8,128)(2,1)}), bf16[4,64,1024]{2,1,0:T(8,128)(2,1)S(1)}, u32[]{:S(2)}, u32[]{:S(2)}) async-start(bf16[4,64,1024]{2,1,0:T(8,128)(2,1)} %broadcast_in_dim.71), calls=%async_computation | async-start | bytes 1048576 | tf_op jit(solution)/shard_map/while/body/eval_jaxpr/all_to_all | solution.py:15
  470.9 3.1 collective-permute-start
  474.1 5.3 copy-start.3
  474.3 31.9 %copy-start.1 = (f32[4096]{0:T(1024)S(1)}, f32[4096]{0:T(1024)}, u32[]{:S(2)}) copy-start(f32[4096]{0:T(1024)} %param.16) | copy-start | bytes 49156
  475.8 29.9 %all-to-all-start.2 = ((bf16[4,256,1024]{1,2,0:T(8,128)(2,1)}), bf16[4,256,1024]{1,2,0:T(8,128)(2,1)S(1)}, u32[]{:S(2)}, u32[]{:S(2)}) async-start(bf16[4,256,1024]{1,2,0:T(8,128)(2,1)} %broadcast_in_dim.59), calls=%async_computation.2 | async-start | bytes 4194304 | tf_op jit(solution)/shard_map/all_to_all | solution.py:15
  525.6 25.6 %copy-start.4 = (f32[4,64]{1,0:T(4,128)S(1)}, f32[4,64]{1,0:T(4,128)}, u32[]{:S(2)}) copy-start(f32[4,64]{1,0:T(4,128)} %param.20) | copy-start | bytes 3076
  525.6 25.6 %copy-start.5 = (s32[4,64]{1,0:T(4,128)S(1)}, s32[4,64]{1,0:T(4,128)}, u32[]{:S(2)}) copy-start(s32[4,64]{1,0:T(4,128)} %param.19) | copy-start | bytes 3076
  525.6 31.4 %copy-start.6 = (s32[1,4]{1,0:T(1,128)S(1)}, s32[1,4]{1,0:T(1,128)}, u32[]{:S(2)}) copy-start(s32[1,4]{1,0:T(1,128)} %param.21) | copy-start | bytes 52
  551.2 13.5 %copy-start.2 = (f32[4,64]{1,0:T(4,128)}, f32[4,64]{1,0:T(4,128)S(1)}, u32[]{:S(2)}) copy-start(f32[4,64]{1,0:T(4,128)S(1)} %reshape.83) | copy-start | bytes 3076
  551.9 11.4 %all-to-all-start.4 = ((f32[16,1,4]{2,1,0:T(1,128)}), f32[16,1,4]{2,1,0:T(1,128)S(1)}, u32[]{:S(2)}, u32[]{:S(2)}) async-start(f32[16,1,4]{2,1,0:T(1,128)} %broadcast_in_dim.62), calls=%async_computation.4 | async-start | bytes 16384 | tf_op jit(solution)/shard_map/all_to_all | solution.py:15
Sparse Core Ops, SparseCore 0:
  10.1 111.0 all-gather.4
  123.4 101.0 all-gather.2
where the time goes:
time: 573 us; the launch traced here: 572 us
  waiting for transfers between devices  289 us (50%)
  blocking collectives  104 us (18%)
  matrix products  91.9 us (16%)
  starting transfers between devices  37.7 us (7%)
  other arithmetic  14.5 us (3%)
  between operations  14.2 us (2%)
  local copies, waits for them, and re-layouts  10.8 us (2%)
  loops' own time  9.23 us (2%)
    all_gather x1, waiting for transfers between devices, shards(): lax.all_gather(down_weight, 'dp', axis=2, tiled=True)  113 us
    all_gather x1, waiting for transfers between devices, shards(): lax.all_gather(up_weight, 'dp', axis=1, tiled=True)  103 us
    all_to_all x5, blocking collectives, sent_and_summed(): lax.all_to_all(parts, axis, split_axis=0, concat_axis=0, tiled=True)  81.6 us
    dot_general x5, matrix products, layer_partial(): jnp.dot(active, down_matrix, preferred_element_type=jnp.float32)  74.3 us
    all_to_all x7, waiting for transfers between devices, copy_for_each(): return lax.all_to_all(copies, axis, split_axis=0, concat_axis=0, tiled=True)  72.2 us
    all_to_all x7, starting transfers between devices, copy_for_each(): return lax.all_to_all(copies, axis, split_axis=0, concat_axis=0, tiled=True)  26.5 us
    dot_general x1, matrix products, shards(): lax.dot_general(normed_final, unembedding, (((1,), (1,)), ((), ())), pref...  17.6 us
    pmax x1, blocking collectives, shards(): top_value = lax.pmax(local_top, ('pipe', 'mp'))  14.3 us
  transfers between devices with their start and end apart: 14, of which 9 were waited for; matrix products, arithmetic and copies ran while one was open for 1% of the time, Pallas kernels for 0%

commit v1 on v0

v1 whole, which is shorter than its diff:
```python
import jax
import jax.numpy as jnp
from jax import lax
from jax.experimental import pallas as pl
from jax.experimental.pallas import tpu as pltpu
from jax.sharding import PartitionSpec as P

epsilon = 1e-05
ipo_tau = 0.5

NX, NY, NZ = 4, 4, 4
D = 4096
FF_DEV = 1792
BLK = 256
TILE_D = 4 * BLK
NH = 2
CHUNKS = ((0, 256), (256, 512), (768, 512), (1280, 512))
NC = len(CHUNKS)
UROWS = 512
NSLOT = 6
V_DEV = 4096
NU = V_DEV // UROWS
NSEM = 480

f32 = jnp.float32
bf16 = jnp.bfloat16


def body(
    hs, up, down, lgain, fgain, unemb, ids, mask,
    o_tok, o_cnt,
    wu, wd, xt, xg, pp, rz1, rz2, ag, yacc, yp, ry1, ry2, sh, xf, xn, ub,
    ssb, ssr, rcol, st, cx, cz, m_s, s_s, k_s,
    sems, usem, gate,
):
    p = lax.axis_index("pipe")
    dp = lax.axis_index("dp")
    y = lax.axis_index("mp")
    x = lax.div(dp, 4)
    z = lax.rem(dp, 4)

    def wrap(v):
        return lax.rem(v + 4, 4)

    xr = [wrap(x + d) for d in range(4)]
    yr = [wrap(y + d) for d in range(4)]
    zr = [wrap(z + d) for d in range(4)]

    def dev(pi, xi, zi, yi):
        return {"pipe": pi, "dp": xi * 4 + zi, "mp": yi}

    names = {}

    def sem(key):
        if key not in names:
            assert len(names) < NSEM
            names[key] = len(names)
        return sems.at[names[key]]

    pending = []

    def send(src, dst, key, to, cond=None):
        cp = pltpu.make_async_remote_copy(
            src_ref=src() if callable(src) else src, dst_ref=dst, send_sem=sem(("s", key)), recv_sem=sem(("r", key)),
            device_id=to, device_id_type=pl.DeviceIdType.MESH,
        )
        cp.start()
        pending.append((src, ("s", key), cond))

    def wait(dst, key):
        pltpu.make_async_copy(dst, dst, sem(("r", key))).wait()

    xp, xm, x2 = xr[1], xr[3], xr[2]
    zp, zm, z2 = zr[1], zr[3], zr[2]
    yq, ym, y2 = yr[1], yr[3], yr[2]
    other = 1 - p
    first = p == 0
    second = p == 1

    def ucopy(k):
        slot = lax.rem(k, NSLOT)
        return pltpu.make_async_copy(
            unemb.at[pl.ds(k * UROWS, UROWS)], ub.at[slot], usem.at[slot]
        )

    xrow = pl.ds(pl.multiple_of(x * BLK, BLK), BLK)
    lw = pltpu.make_async_copy(up, wu.at[xrow, :], sem("lwu"))
    lw.start()
    ld = pltpu.make_async_copy(down, wd.at[:, xrow], sem("lwd"))
    ld.start()

    cols_of = [
        [pl.ds(pl.multiple_of((xb * 4 + zr[d]) * BLK, BLK), BLK) for d in range(4)]
        for xb in range(4)
    ]

    def hcols(xb, d):
        return cols_of[xb][d]

    cx[...] = jnp.zeros_like(cx)
    cz[...] = jnp.zeros_like(cz)

    bar = pltpu.get_barrier_semaphore()
    peers = []
    for d in (1, 2, 3):
        peers.append(dev(p, xr[d], z, y))
        peers.append(dev(p, x, zr[d], y))
        peers.append(dev(p, x, z, yr[d]))
    for d in range(4):
        peers.append(dev(other, x, z, yr[d]))
    for peer in peers:
        pl.semaphore_signal(bar, inc=1, device_id=peer, device_id_type=pl.DeviceIdType.MESH)
    pl.semaphore_wait(bar, len(peers))

    items = [("u", c) for c in range(NC)] + [("d", c) for c in range(NC)]

    def own_weights(i):
        kind, c = items[i]
        o, w = CHUNKS[c]
        if kind == "u":
            src = up.at[:, pl.ds(o, w)]
            dst = wu.at[xrow, pl.ds(o, w)]
        else:
            src = down.at[pl.ds(o, w), :]
            dst = wd.at[pl.ds(o, w), xrow]
        return src, dst

    def wslice(i, xb, part=None):
        kind, c = items[i]
        o, w = CHUNKS[c]
        if kind == "u":
            n = BLK if part is None else BLK // 2
            s = xb * BLK + (0 if part is None else part * (BLK // 2))
            return wu.at[pl.ds(pl.multiple_of(s, n), n), pl.ds(o, w)]
        n = w if part is None else w // 2
        s = o + (0 if part is None else part * (w // 2))
        return wd.at[pl.ds(s, n), pl.ds(pl.multiple_of(xb * BLK, BLK), BLK)]

    def weights_own(i, cond=None):
        _, dst = own_weights(i)
        src = lambda: own_weights(i)[0]
        if cond is None:
            src = src()
        send(src, dst, ("w", i, 0), dev(p, xp, z, y), cond)
        send(src, dst, ("w", i, 1), dev(p, xm, z, y), cond)

    def weights_forward(i):
        a = wslice(i, xm)
        wait(a, ("w", i, 0))
        h = wslice(i, xm, 0)
        send(h, h, ("w", i, 2), dev(p, xp, z, y))
        b = wslice(i, xp)
        wait(b, ("w", i, 1))
        h = wslice(i, xp, 1)
        send(h, h, ("w", i, 3), dev(p, xm, z, y))
        if i + 2 < len(items):
            weights_own(i + 2)
        if i == len(items) - 3:
            @pl.when(first)
            def _():
                pl.semaphore_signal(gate, inc=1, device_id=dev(1, x, z, y),
                                    device_id_type=pl.DeviceIdType.MESH)

    def weights_last(i):
        wait(wslice(i, x2, 0), ("w", i, 2))
        wait(wslice(i, x2, 1), ("w", i, 3))

    @pl.when(first)
    def _():
        weights_own(0, first)
        weights_own(1, first)
        for h in range(NH):
            for d in (1, 3, 2):
                zt = zr[d]
                for xb in range(4):
                    send(
                        lambda h=h, d=d, xb=xb: hs.at[h, :, :, hcols(xb, d)],
                        xt.at[h, :, z, :, pl.ds(xb * BLK, BLK)],
                        ("x", h, d, xb), dev(0, x, zt, y), first,
                    )
            for xb in range(4):
                pltpu.make_async_copy(
                    hs.at[h, :, :, hcols(xb, 0)], xt.at[h, :, z, :, pl.ds(xb * BLK, BLK)],
                    sem(("xl", h, xb)),
                ).start()

    for k in range(NSLOT):
        ucopy(k).start()

    own = jnp.sum(mask[...].astype(f32), axis=1, keepdims=True)
    cx[x, 0:4, :] = jnp.broadcast_to(own, (4, 128))
    for d in (1, 2, 3):
        send(cx.at[x], cx.at[x], ("cx", d), dev(p, xr[d], z, y))

    @pl.when(second)
    def _():
        pl.semaphore_wait(gate, 1)
        weights_own(0, second)
        weights_own(1, second)

    gz = jnp.concatenate([lgain[:, hcols(xb, 0)] for xb in range(4)], axis=1)

    def tile_arrived(h):
        @pl.when(first)
        def _():
            for xb in range(4):
                pltpu.make_async_copy(
                    hs.at[h, :, :, hcols(xb, 0)], xt.at[h, :, z, :, pl.ds(xb * BLK, BLK)],
                    sem(("xl", h, xb)),
                ).wait()
            for d in (1, 3, 2):
                zs = zr[(4 - d) % 4]
                for xb in range(4):
                    wait(xt.at[h, :, zs, :, pl.ds(xb * BLK, BLK)], ("x", h, d, xb))

        @pl.when(second)
        def _():
            wait(xt.at[h, ym], ("g", h, 0))
            a = lambda: xt.at[h, ym, 0:2]
            send(a, a(), ("g", h, 3), dev(1, x, z, yq), second)
            wait(xt.at[h, yq], ("g", h, 1))
            b = lambda: xt.at[h, yq, 2:4]
            send(b, b(), ("g", h, 4), dev(1, x, z, ym), second)
            wait(xt.at[h, y], ("g", h, 2))
            wait(xt.at[h, y2, 0:2], ("g", h, 3))
            wait(xt.at[h, y2, 2:4], ("g", h, 4))

    def tile_ready(h):
        tile_arrived(h)
        ones = jnp.ones((8, TILE_D), bf16)
        for g in range(4):
            v = xt[h, :, g].reshape(128, TILE_D).astype(f32)
            xg[h, :, g] = (v * gz).astype(bf16).reshape(4, 32, TILE_D)
            sq = v * v
            hi = sq.astype(bf16)
            lo = (sq - hi.astype(f32)).astype(bf16)
            dn = (((1,), (1,)), ((), ()))
            ssb[h, g] = lax.dot_general(
                ones, hi, dn, preferred_element_type=f32
            ) + lax.dot_general(ones, lo, dn, preferred_element_type=f32)
        for d in (1, 3, 2):
            zt = zr[d]
            send(ssb.at[h, zt], ssr.at[h, d - 1], ("ss", h, d), dev(p, x, zt, y))

    def row_scale(h):
        for d in (1, 3, 2):
            wait(ssr.at[h, d - 1], ("ss", h, d))
        total = ssb[h, z] + ssr[h, 0] + ssr[h, 1] + ssr[h, 2]
        scale = lax.rsqrt(total * (1.0 / D) + epsilon)
        col = jnp.transpose(scale, (1, 0))[:, 0:1]
        rcol[h] = jnp.broadcast_to(col, (128, 128))

    def up_chunk(h, c):
        o, w = CHUNKS[c]
        lhs = xg[h].reshape(512, TILE_D)
        for n in range(o, o + w, 256):
            r = jnp.dot(lhs, wu[:, n : n + 256], preferred_element_type=f32)
            pp[h, :, :, :, n : n + 256] = r.astype(bf16).reshape(4, 4, 32, 256)
        cs = pl.ds(o, w)
        send(pp.at[h, 0:2, z2, :, cs], rz1.at[h, 0, :, :, cs], ("z1", h, c, 0), dev(p, x, zp, y))
        send(pp.at[h, 2:4, z2, :, cs], rz1.at[h, 1, :, :, cs], ("z1", h, c, 1), dev(p, x, zm, y))
        send(pp.at[h, 2:4, zp, :, cs], rz2.at[h, 0, 2:4, :, cs], ("z2", h, c, 0), dev(p, x, zp, y))
        send(pp.at[h, 0:2, zm, :, cs], rz2.at[h, 1, 0:2, :, cs], ("z2", h, c, 1), dev(p, x, zm, y))

    def reduce_one(h, c):
        o, w = CHUNKS[c]
        cs = pl.ds(o, w)
        wait(rz1.at[h, 0, :, :, cs], ("z1", h, c, 0))
        pp[h, 0:2, zp, :, cs] = (
            pp[h, 0:2, zp, :, cs].astype(f32) + rz1[h, 0, :, :, cs].astype(f32)
        ).astype(bf16)
        send(pp.at[h, 0:2, zp, :, cs], rz2.at[h, 0, 0:2, :, cs], ("z2", h, c, 2), dev(p, x, zp, y))
        wait(rz1.at[h, 1, :, :, cs], ("z1", h, c, 1))
        pp[h, 2:4, zm, :, cs] = (
            pp[h, 2:4, zm, :, cs].astype(f32) + rz1[h, 1, :, :, cs].astype(f32)
        ).astype(bf16)
        send(pp.at[h, 2:4, zm, :, cs], rz2.at[h, 1, 2:4, :, cs], ("z2", h, c, 3), dev(p, x, zm, y))

    def reduce_two(h, c):
        o, w = CHUNKS[c]
        cs = pl.ds(o, w)
        if c == 0:
            row_scale(h)
        wait(rz2.at[h, 0, 2:4, :, cs], ("z2", h, c, 0))
        wait(rz2.at[h, 1, 0:2, :, cs], ("z2", h, c, 1))
        wait(rz2.at[h, 0, 0:2, :, cs], ("z2", h, c, 2))
        wait(rz2.at[h, 1, 2:4, :, cs], ("z2", h, c, 3))
        s = (
            pp[h, :, z, :, cs].astype(f32)
            + rz2[h, 0, :, :, cs].astype(f32)
            + rz2[h, 1, :, :, cs].astype(f32)
        ).reshape(128, w)
        v = s * rcol[h][:, 0:1]
        act = v / (1.0 + jnp.exp(-v))
        ag[h, :, z, :, cs] = act.astype(bf16).reshape(4, 32, w)
        a = ag.at[h, :, z, :, cs]
        send(a, a, ("a", h, c, 0), dev(p, x, zp, y))
        send(a, a, ("a", h, c, 1), dev(p, x, zm, y))

    def gather_one(h, c):
        o, w = CHUNKS[c]
        cs = pl.ds(o, w)
        wait(ag.at[h, :, zm, :, cs], ("a", h, c, 0))
        a = ag.at[h, 0:2, zm, :, cs]
        send(a, a, ("a", h, c, 2), dev(p, x, zp, y))
        wait(ag.at[h, :, zp, :, cs], ("a", h, c, 1))
        b = ag.at[h, 2:4, zp, :, cs]
        send(b, b, ("a", h, c, 3), dev(p, x, zm, y))

    def down_chunk(h, c):
        o, w = CHUNKS[c]
        cs = pl.ds(o, w)
        wait(ag.at[h, 0:2, z2, :, cs], ("a", h, c, 2))
        wait(ag.at[h, 2:4, z2, :, cs], ("a", h, c, 3))
        lhs = ag[h, :, :, :, cs].reshape(512, w)
        for n in range(0, TILE_D, 256):
            r = jnp.dot(lhs, wd[cs, n : n + 256], preferred_element_type=f32)
            if c > 0:
                r = r + yacc[:, n : n + 256]
            if c == NC - 1:
                yp[h, :, :, :, n : n + 256] = r.astype(bf16).reshape(4, 4, 32, 256)
            else:
                yacc[:, n : n + 256] = r

    def y_start(h):
        send(yp.at[h, y2, 0:2], ry1.at[h, 0], ("y1", h, 0), dev(p, x, z, yq))
        send(yp.at[h, y2, 2:4], ry1.at[h, 1], ("y1", h, 1), dev(p, x, z, ym))
        send(yp.at[h, yq, 2:4], ry2.at[h, 0, 2:4], ("y2", h, 0), dev(p, x, z, yq))
        send(yp.at[h, ym, 0:2], ry2.at[h, 1, 0:2], ("y2", h, 1), dev(p, x, z, ym))

    def y_mid(h):
        wait(ry1.at[h, 0], ("y1", h, 0))
        yp[h, yq, 0:2] = (yp[h, yq, 0:2].astype(f32) + ry1[h, 0].astype(f32)).astype(bf16)
        send(yp.at[h, yq, 0:2], ry2.at[h, 0, 0:2], ("y2", h, 2), dev(p, x, z, yq))
        wait(ry1.at[h, 1], ("y1", h, 1))
        yp[h, ym, 2:4] = (yp[h, ym, 2:4].astype(f32) + ry1[h, 1].astype(f32)).astype(bf16)
        send(yp.at[h, ym, 2:4], ry2.at[h, 1, 2:4], ("y2", h, 3), dev(p, x, z, ym))

    def y_end(h):
        wait(ry2.at[h, 0, 2:4], ("y2", h, 0))
        wait(ry2.at[h, 1, 0:2], ("y2", h, 1))
        wait(ry2.at[h, 0, 0:2], ("y2", h, 2))
        wait(ry2.at[h, 1, 2:4], ("y2", h, 3))
        sh[h] = (
            xt[h, y].astype(f32) + yp[h, y].astype(f32) + ry2[h, 0].astype(f32) + ry2[h, 1].astype(f32)
        ).astype(bf16)

        @pl.when(first)
        def _():
            dst = xt.at[h, y]
            send(lambda: sh.at[h], dst, ("g", h, 0), dev(1, x, z, yq), first)
            send(lambda: sh.at[h], dst, ("g", h, 1), dev(1, x, z, ym), first)
            send(lambda: sh.at[h], dst, ("g", h, 2), dev(1, x, z, y), first)

        @pl.when(second)
        def _():
            for d in (1, 3, 2):
                zt = zr[d]
                for xb in range(4):
                    send(
                        lambda d=d, xb=xb: sh.at[h, zr[d], :, pl.ds(xb * BLK, BLK)],
                        xf.at[h, y, :, hcols(xb, 0)],
                        ("f", h, d, xb), dev(1, x, zt, y), second,
                    )
            for xb in range(4):
                xf[h, y, :, hcols(xb, 0)] = sh[h, z, :, xb * BLK : (xb + 1) * BLK]

    half_d = D // 2

    def finals_one(h):
        @pl.when(second)
        def _():
            for d in (1, 3, 2):
                zs = zr[(4 - d) % 4]
                for xb in range(4):
                    wait(xf.at[h, y, :, hcols(xb, (4 - d) % 4)], ("f", h, d, xb))
            a = lambda: xf.at[h, y]
            send(a, a(), ("q", h, 0), dev(1, x, z, yq), second)
            send(a, a(), ("q", h, 1), dev(1, x, z, ym), second)
            send(a, a(), ("q", h, 4), dev(0, x, z, y), second)

    def finals_two(h):
        @pl.when(second)
        def _():
            wait(xf.at[h, ym], ("q", h, 0))
            a = lambda: xf.at[h, ym, :, pl.ds(0, half_d)]
            send(a, a(), ("q", h, 2), dev(1, x, z, yq), second)
            wait(xf.at[h, yq], ("q", h, 1))
            b = lambda: xf.at[h, yq, :, pl.ds(half_d, half_d)]
            send(b, b(), ("q", h, 3), dev(1, x, z, ym), second)
            e = lambda: xf.at[h, ym]
            send(e, e(), ("q", h, 5), dev(0, x, z, y), second)
            f = lambda: xf.at[h, yq]
            send(f, f(), ("q", h, 6), dev(0, x, z, y), second)

    def finals_three(h):
        @pl.when(second)
        def _():
            wait(xf.at[h, y2, :, pl.ds(0, half_d)], ("q", h, 2))
            wait(xf.at[h, y2, :, pl.ds(half_d, half_d)], ("q", h, 3))
            a = lambda: xf.at[h, y2]
            send(a, a(), ("q", h, 7), dev(0, x, z, y), second)

        @pl.when(first)
        def _():
            wait(xf.at[h, y], ("q", h, 4))
            wait(xf.at[h, ym], ("q", h, 5))
            wait(xf.at[h, yq], ("q", h, 6))
            wait(xf.at[h, y2], ("q", h, 7))

    def final_norm(h):
        for q in range(4):
            v = xf[h, q].astype(f32)
            r = lax.rsqrt(jnp.mean(v * v, axis=1, keepdims=True) + epsilon)
            xn[pl.ds(h * 128 + q * 32, 32), :] = (v * r * fgain[...]).astype(bf16)

    steps = [(h, c) for h in range(NH) for c in range(NC)]
    lw.wait()
    ld.wait()

    def y_tail(h, stage):
        if stage == 0:
            y_start(h)
        elif stage == 1:
            y_mid(h)
        else:
            y_end(h)

    n = len(steps)
    y_events = {}
    for i in range(n + NC + 8):
        if i < len(items):
            weights_forward(i)
        if i - 1 >= 0 and i - 1 < n:
            reduce_one(*steps[i - 1])
        if i - 2 >= 0 and i - 2 < n:
            reduce_two(*steps[i - 2])
        if i - 3 >= 0 and i - 3 < n:
            gather_one(*steps[i - 3])
        if i < n:
            h, c = steps[i]
            if h == 0:
                weights_last(i)
            if c == 0:
                tile_ready(h)
            up_chunk(h, c)
        j = i - NC - 1
        if 0 <= j < n:
            h, c = steps[j]
            if h == 0:
                weights_last(NC + c)
            down_chunk(h, c)
            if c == NC - 1:
                y_start(h)
                y_events.setdefault(i + 1, []).append((y_mid, h))
                y_events.setdefault(i + 2, []).append((y_end, h))
                y_events.setdefault(i + 3, []).append((finals_one, h))
        for f, h in y_events.pop(i, []):
            f(h)
    assert not y_events
    for h in range(NH):
        finals_two(h)
        finals_three(h)
        final_norm(h)

    for d in (1, 2, 3):
        wait(cx.at[xr[(4 - d) % 4]], ("cx", d))
    cz[z] = cx[0] + cx[1] + cx[2] + cx[3]
    for d in (1, 2, 3):
        send(cz.at[z], cz.at[z], ("cz", d), dev(p, x, zr[d], y))

    m_s[...] = jnp.full_like(m_s, -jnp.inf)
    s_s[...] = jnp.zeros_like(s_s)
    k_s[...] = jnp.zeros_like(k_s)
    vocab_index = p * 4 + y

    def head(k, carry):
        slot = lax.rem(k, NSLOT)
        ucopy(k).wait()
        lt = lax.dot_general(
            ub[slot], xn[...], (((1,), (1,)), ((), ())), preferred_element_type=f32
        )
        m_old = m_s[0:1, :]
        m_new = jnp.maximum(m_old, jnp.max(lt, axis=0, keepdims=True))
        rows = lax.broadcasted_iota(jnp.int32, lt.shape, 0) + (vocab_index * V_DEV + k * UROWS)
        k_s[0:1, :] = k_s[0:1, :] + jnp.sum(
            jnp.where(rows == ids[...], lt, 0.0), axis=0, keepdims=True
        )
        s_s[0:1, :] = s_s[0:1, :] * jnp.exp(m_old - m_new) + jnp.sum(
            jnp.exp(lt - m_new), axis=0, keepdims=True
        )
        m_s[0:1, :] = m_new

        @pl.when(k + NSLOT < NU)
        def _():
            ucopy(k + NSLOT).start()

        return carry

    lax.fori_loop(0, NU, head, 0)

    st[vocab_index, 0:8] = m_s[...]
    st[vocab_index, 8:16] = s_s[...]
    st[vocab_index, 16:24] = k_s[...]
    mine = st.at[vocab_index]
    for d in range(4):
        yt = yr[d]
        if d > 0:
            send(mine, mine, ("st", 0, d), dev(p, x, z, yt))
        send(mine, mine, ("st", 1, d), dev(other, x, z, yt))
    for d in range(4):
        ys = yr[(4 - d) % 4]
        if d > 0:
            wait(st.at[p * 4 + ys], ("st", 0, d))
        wait(st.at[other * 4 + ys], ("st", 1, d))
    ms = [st[i, 0:8] for i in range(8)]
    top = ms[0]
    for i in range(1, 8):
        top = jnp.maximum(top, ms[i])
    tot = jnp.zeros_like(top)
    pick = jnp.zeros_like(top)
    for i in range(8):
        tot = tot + st[i, 8:16] * jnp.exp(ms[i] - top)
        pick = pick + st[i, 16:24]
    o_tok[...] = pick - top - jnp.log(tot)

    for d in (1, 2, 3):
        wait(cz.at[zr[(4 - d) % 4]], ("cz", d))
    o_cnt[...] = cz[0] + cz[1] + cz[2] + cz[3]

    for src, ssem, cond in pending:
        if cond is None:
            pltpu.make_async_copy(src, src, sem(ssem)).wait()
    for which in (first, second):
        @pl.when(which)
        def _():
            for src, ssem, cond in pending:
                if cond is which:
                    ref = src()
                    pltpu.make_async_copy(ref, ref, sem(ssem)).wait()


def run(hs, up, down, lgain, fgain, unemb, ids, mask):
    anyspace = pl.BlockSpec(memory_space=pltpu.HBM)
    vm = pl.BlockSpec(memory_space=pltpu.VMEM)
    V = pltpu.VMEM
    return pl.pallas_call(
        body,
        out_shape=(
            jax.ShapeDtypeStruct((8, 256), f32),
            jax.ShapeDtypeStruct((8, 128), f32),
        ),
        in_specs=[anyspace, anyspace, anyspace, vm, vm, anyspace, vm, vm],
        out_specs=(vm, vm),
        scratch_shapes=[
            V((TILE_D, FF_DEV), bf16),
            V((FF_DEV, TILE_D), bf16),
            V((NH, 4, 4, 32, TILE_D), bf16),
            V((NH, 4, 4, 32, TILE_D), bf16),
            V((NH, 4, 4, 32, FF_DEV), bf16),
            V((NH, 2, 2, 32, FF_DEV), bf16),
            V((NH, 2, 4, 32, FF_DEV), bf16),
            V((NH, 4, 4, 32, FF_DEV), bf16),
            V((512, TILE_D), f32),
            V((NH, 4, 4, 32, TILE_D), bf16),
            V((NH, 2, 2, 32, TILE_D), bf16),
            V((NH, 2, 4, 32, TILE_D), bf16),
            V((NH, 4, 32, TILE_D), bf16),
            V((NH, 4, 32, D), bf16),
            V((256, D), bf16),
            V((NSLOT, UROWS, D), bf16),
            V((NH, 4, 8, 128), f32),
            V((NH, 3, 8, 128), f32),
            V((NH, 128, 128), f32),
            V((8, 24, 256), f32),
            V((4, 8, 128), f32),
            V((4, 8, 128), f32),
            V((8, 256), f32),
            V((8, 256), f32),
            V((8, 256), f32),
            pltpu.SemaphoreType.DMA((NSEM,)),
            pltpu.SemaphoreType.DMA((NSLOT,)),
            pltpu.SemaphoreType.REGULAR,
        ],
        compiler_params=pltpu.CompilerParams(
            collective_id=0, has_side_effects=True, vmem_limit_bytes=66_000_000
        ),
        name="relay",
    )(hs, up, down, lgain, fgain, unemb, ids, mask)


def shards(
    hidden_states, up_weight, down_weight, layer_gain, final_gain, unembedding,
    target_ids, response_masks, anchor_logps, pairing,
):
    tok, cnt = run(
        hidden_states.reshape(NH, 4, 32, D),
        up_weight[0],
        down_weight[0],
        layer_gain,
        final_gain.reshape(1, D),
        unembedding,
        target_ids.reshape(1, 256),
        response_masks,
    )
    token_logps = tok[0].reshape(4, 64)
    counts = cnt[0:4, 0]
    mask_values = response_masks.astype(f32)
    divisor = counts / 16.0
    policy = jnp.sum(mask_values * token_logps, axis=1) / divisor
    anchor = jnp.sum(mask_values * anchor_logps, axis=1) / divisor
    log_gaps = policy - anchor
    positions = jnp.arange(4, dtype=jnp.int32)
    chosen = jnp.sum(
        jnp.where(pairing[0, 0::2][:, None] == positions[None, :], log_gaps[None, :], 0.0), axis=1
    )
    rejected = jnp.sum(
        jnp.where(pairing[0, 1::2][:, None] == positions[None, :], log_gaps[None, :], 0.0), axis=1
    )
    losses = (chosen - rejected - 0.5 / ipo_tau) ** 2
    return (token_logps, policy, losses)


def solution(mesh):
    return jax.shard_map(
        shards,
        mesh=mesh,
        in_specs=(
            P("dp", None, None),
            P("pipe", "dp", "mp"),
            P("pipe", "mp", "dp"),
            P("pipe", None),
            P(),
            P(("pipe", "mp"), None),
            P("dp", None),
            P("dp", None),
            P("dp", None),
            P("dp", None),
        ),
        out_specs=(P("dp", None), P("dp"), P("dp")),
        check_vma=False,
    )
```

time: 573 us -> 192 us (0.34)
  waiting for transfers between devices: 289 us -> 0 us
  Pallas kernels: 0 us -> 186 us
  blocking collectives: 104 us -> 0 us
  matrix products: 91.9 us -> 0 us
  starting transfers between devices: 37.7 us -> 0 us
  between operations: 14.2 us -> 0.67 us
  other arithmetic: 14.5 us -> 2.2 us
  loops' own time: 9.23 us -> 0 us
  local copies, waits for them, and re-layouts: 10.8 us -> 2.34 us
    all_gather x2 -> x0, waiting for transfers between devices: 216 us -> none  [the longest x1 113 us: shards(): lax.all_gather(down_weight, 'dp', axis=2, tiled=True)]
    pallas_call x0 -> x1, Pallas kernels: none -> 186 us  [run(): pl.pallas_call(body, out_shape=(jax.ShapeDtypeStruct((8, 256), f32), jax....]
    dot_general x6 -> x0, matrix products: 91.9 us -> none  [the longest x5 74.3 us: layer_partial(): jnp.dot(active, down_matrix, preferred_element_type=jnp.float32)]
    all_to_all x6 -> x0, blocking collectives: 89.4 us -> none  [the longest x5 81.6 us: sent_and_summed(): lax.all_to_all(parts, axis, split_axis=0, concat_axis=0, tiled=True)]
    all_to_all x7 -> x0, waiting for transfers between devices: 72.2 us -> none  [copy_for_each(): return lax.all_to_all(copies, axis, split_axis=0, concat_axis=0, tiled=True)]
    all_to_all x7 -> x0, starting transfers between devices: 26.5 us -> none  [copy_for_each(): return lax.all_to_all(copies, axis, split_axis=0, concat_axis=0, tiled=True)]
    pmax x1 -> x0, blocking collectives: 14.3 us -> none  [shards(): top_value = lax.pmax(local_top, ('pipe', 'mp'))]
    ppermute x5 -> x0, starting transfers between devices: 11.2 us -> none  [from_behind(): return lax.ppermute(value, axis, pairs)]
  transfers between devices with their start and end apart: 14 -> 0, of which waited for: 9 -> 0; matrix products, arithmetic and copies ran while one was open for 1% -> 0% of each run, Pallas kernels for 0% -> 0%
where the time goes in v1:
time: 192 us
  Pallas kernels  186 us (97%)
  local copies, waits for them, and re-layouts  2.34 us (1%)
  other arithmetic  2.2 us (1%)
    pallas_call x1, Pallas kernels, run(): pl.pallas_call(body, out_shape=(jax.ShapeDtypeStruct((8, 256), f32), jax....  186 us

profile of v1, /device:TPU:1, one launch (start us, length us, event | category | flops | bytes accessed | tf_op | source)
XLA Modules:
  0.0 191.7 jit_solution(12310634969618716711)
XLA Ops:
  0.6 0.0 copy-start
  0.6 0.0 copy-start.2
  0.7 0.0 copy-start.3
  0.7 1.3 reshape.33.ids
  2.0 186.5 %relay.1 = (f32[8,256]{1,0:T(8,128)}, f32[8,128]{1,0:T(8,128)}) custom-call(bf16[2,4,32,4096]{3,2,1,0:T(8,128)(2,1)} %bitcast.6, bf16[256,1792]{1,0:T(8,128)(2,1)} %bitcast.7, bf16[1792,256]{1,0:T(8,128)(2,1)} %bitcast.8, f32[1,4096]{1,0:T(1,128)} %lgain.1, f32[1,4096]{1,0:T(1,128)} %bitcast.9, bf16[4096,4096]{1,0:T(8,128)(2,1)} %unemb.1, ...), custom_call_target="tpu_custom_call" | custom-call | tf_op jit(solution)/shard_map/relay/pallas_call | solution.py:547
  188.5 0.7 slice_reduce_fusion
  189.2 0.1 reshape_squeeze.3
  189.3 0.0 copy-done
  189.3 0.0 copy-done.2
  189.3 0.0 copy-start.1
  189.3 0.1 multiply_reduce_fusion
  189.4 0.8 multiply_reduce_fusion.1
  190.2 0.5 divide_subtract_fusion
  190.8 0.0 copy-done.3
  190.8 0.1 slice.14
  190.9 0.1 slice.15
  191.0 0.2 fusion.1
  191.2 0.5 add_multiply_fusion
  191.7 0.0 copy-done.1
Async XLA Ops:
  0.6 188.7 %copy-start = (s32[4,64]{1,0:T(4,128)S(1)}, s32[4,64]{1,0:T(4,128)}, u32[]{:S(2)}) copy-start(s32[4,64]{1,0:T(4,128)} %mask.1) | copy-start | bytes 3076
  0.6 188.7 %copy-start.2 = (f32[4,64]{1,0:T(4,128)S(1)}, f32[4,64]{1,0:T(4,128)}, u32[]{:S(2)}) copy-start(f32[4,64]{1,0:T(4,128)} %param.18) | copy-start | bytes 3076
  0.7 190.1 %copy-start.3 = (s32[1,4]{1,0:T(1,128)S(1)}, s32[1,4]{1,0:T(1,128)}, u32[]{:S(2)}) copy-start(s32[1,4]{1,0:T(1,128)} %param.19) | copy-start | bytes 52
  189.3 2.4 %copy-start.1 = (f32[4,64]{1,0:T(4,128)}, f32[4,64]{1,0:T(4,128)S(1)}, u32[]{:S(2)}) copy-start(f32[4,64]{1,0:T(4,128)S(1)} %reshape_squeeze.3) | copy-start | bytes 3076

commit v2 on v1

--- a/solution.py
+++ b/solution.py
@@ -13,14 +13,23 @@
 FF_DEV = 1792
 BLK = 256
 TILE_D = 4 * BLK
-NH = 2
+NH = 4
+R = 32 // (NH // 2)
+AHEAD = 2
+WF_SLOT = (-1, 0, 2, 4, 6, 8, 10, 12)
+GATE = 0
+PRE = 4
 CHUNKS = ((0, 256), (256, 512), (768, 512), (1280, 512))
+LAG = 2
 NC = len(CHUNKS)
 UROWS = 512
 NSLOT = 6
 V_DEV = 4096
 NU = V_DEV // UROWS
-NSEM = 480
+NS = 1
+SUB = TILE_D // NS
+XB = 4 // NS
+NSEM = 1200
 
 f32 = jnp.float32
 bf16 = jnp.bfloat16
@@ -87,7 +96,6 @@
     lw = pltpu.make_async_copy(up, wu.at[xrow, :], sem("lwu"))
     lw.start()
     ld = pltpu.make_async_copy(down, wd.at[:, xrow], sem("lwd"))
-    ld.start()
 
     cols_of = [
         [pl.ds(pl.multiple_of((xb * 4 + zr[d]) * BLK, BLK), BLK) for d in range(4)]
@@ -99,6 +107,7 @@
 
     cx[...] = jnp.zeros_like(cx)
     cz[...] = jnp.zeros_like(cz)
+    ssb[...] = jnp.zeros_like(ssb)
 
     bar = pltpu.get_barrier_semaphore()
     peers = []
@@ -110,7 +119,8 @@
         peers.append(dev(other, x, z, yr[d]))
     for peer in peers:
         pl.semaphore_signal(bar, inc=1, device_id=peer, device_id_type=pl.DeviceIdType.MESH)
-    pl.semaphore_wait(bar, len(peers))
+    with jax.named_scope("barrier"):
+        pl.semaphore_wait(bar, len(peers))
 
     items = [("u", c) for c in range(NC)] + [("d", c) for c in range(NC)]
 
@@ -144,48 +154,63 @@
         send(src, dst, ("w", i, 0), dev(p, xp, z, y), cond)
         send(src, dst, ("w", i, 1), dev(p, xm, z, y), cond)
 
-    def weights_forward(i):
-        a = wslice(i, xm)
-        wait(a, ("w", i, 0))
-        h = wslice(i, xm, 0)
-        send(h, h, ("w", i, 2), dev(p, xp, z, y))
-        b = wslice(i, xp)
-        wait(b, ("w", i, 1))
-        h = wslice(i, xp, 1)
-        send(h, h, ("w", i, 3), dev(p, xm, z, y))
-        if i + 2 < len(items):
-            weights_own(i + 2)
-        if i == len(items) - 3:
-            @pl.when(first)
-            def _():
+    def weights_forward(i, cond):
+        @pl.when(cond)
+        def _():
+            wait(wslice(i, xm), ("w", i, 0))
+            a = lambda: wslice(i, xm, 0)
+            send(a, a(), ("w", i, 2), dev(p, xp, z, y), cond)
+            wait(wslice(i, xp), ("w", i, 1))
+            b = lambda: wslice(i, xp, 1)
+            send(b, b(), ("w", i, 3), dev(p, xm, z, y), cond)
+            if cond is first and i == 0:
+                for k in range(2, AHEAD):
+                    weights_own(k, cond)
+            if i + AHEAD < len(items):
+                weights_own(i + AHEAD, cond)
+            if cond is first and i == len(items) - 1 - GATE:
                 pl.semaphore_signal(gate, inc=1, device_id=dev(1, x, z, y),
                                     device_id_type=pl.DeviceIdType.MESH)
 
     def weights_last(i):
         wait(wslice(i, x2, 0), ("w", i, 2))
         wait(wslice(i, x2, 1), ("w", i, 3))
+
+    def far_tokens(h):
+        for xb in range(4):
+            send(
+                lambda h=h, xb=xb: hs.at[h, y, :, hcols(xb, 2)],
+                xt.at[h, y, z, :, pl.ds(xb * BLK, BLK)],
+                ("x", h, 2, xb), dev(0, x, z2, y), first,
+            )
+
+    def near_tokens(h):
+        for d in (1, 3):
+            for xb in range(4):
+                send(
+                    lambda h=h, d=d, xb=xb: hs.at[h, :, :, hcols(xb, d)],
+                    xt.at[h, :, z, :, pl.ds(xb * BLK, BLK)],
+                    ("x", h, d, xb), dev(0, x, zr[d], y), first,
+                )
+        for xb in range(4):
+            pltpu.make_async_copy(
+                hs.at[h, :, :, hcols(xb, 0)], xt.at[h, :, z, :, pl.ds(xb * BLK, BLK)],
+                sem(("xl", h, xb)),
+            ).start()
+
+    def near_later(h):
+        @pl.when(first)
+        def _():
+            near_tokens(h)
 
     @pl.when(first)
     def _():
         weights_own(0, first)
         weights_own(1, first)
         for h in range(NH):
-            for d in (1, 3, 2):
-                zt = zr[d]
-                for xb in range(4):
-                    send(
-                        lambda h=h, d=d, xb=xb: hs.at[h, :, :, hcols(xb, d)],
-                        xt.at[h, :, z, :, pl.ds(xb * BLK, BLK)],
-                        ("x", h, d, xb), dev(0, x, zt, y), first,
-                    )
-            for xb in range(4):
-                pltpu.make_async_copy(
-                    hs.at[h, :, :, hcols(xb, 0)], xt.at[h, :, z, :, pl.ds(xb * BLK, BLK)],
-                    sem(("xl", h, xb)),
-                ).start()
-
-    for k in range(NSLOT):
-        ucopy(k).start()
+            far_tokens(h)
+            if h < 2:
+                near_tokens(h)
 
     own = jnp.sum(mask[...].astype(f32), axis=1, keepdims=True)
     cx[x, 0:4, :] = jnp.broadcast_to(own, (4, 128))
@@ -195,8 +220,8 @@
     @pl.when(second)
     def _():
         pl.semaphore_wait(gate, 1)
-        weights_own(0, second)
-        weights_own(1, second)
+        for i in range(AHEAD):
+            weights_own(i, second)
 
     gz = jnp.concatenate([lgain[:, hcols(xb, 0)] for xb in range(4)], axis=1)
 
@@ -208,34 +233,53 @@
                     hs.at[h, :, :, hcols(xb, 0)], xt.at[h, :, z, :, pl.ds(xb * BLK, BLK)],
                     sem(("xl", h, xb)),
                 ).wait()
-            for d in (1, 3, 2):
+            for d in (1, 3):
                 zs = zr[(4 - d) % 4]
                 for xb in range(4):
                     wait(xt.at[h, :, zs, :, pl.ds(xb * BLK, BLK)], ("x", h, d, xb))
+            for d in (1, 3, 2):
+                wait(xt.at[h, yr[(4 - d) % 4], z2], ("xy", h, d))
 
         @pl.when(second)
         def _():
-            wait(xt.at[h, ym], ("g", h, 0))
-            a = lambda: xt.at[h, ym, 0:2]
-            send(a, a(), ("g", h, 3), dev(1, x, z, yq), second)
-            wait(xt.at[h, yq], ("g", h, 1))
-            b = lambda: xt.at[h, yq, 2:4]
-            send(b, b(), ("g", h, 4), dev(1, x, z, ym), second)
-            wait(xt.at[h, y], ("g", h, 2))
-            wait(xt.at[h, y2, 0:2], ("g", h, 3))
-            wait(xt.at[h, y2, 2:4], ("g", h, 4))
+            for e in range(NS):
+                es = pl.ds(e * SUB, SUB)
+                wait(xt.at[h, y, :, :, es], ("g", h, e, 2))
+                wait(xt.at[h, y2, 0:2, :, es], ("g", h, e, 3))
+                wait(xt.at[h, y2, 2:4, :, es], ("g", h, e, 4))
+
+    def tile_relay_first(h):
+        @pl.when(first)
+        def _():
+            for xb in range(4):
+                wait(xt.at[h, y, z2, :, pl.ds(xb * BLK, BLK)], ("x", h, 2, xb))
+            a = lambda: xt.at[h, y, z2]
+            for d in (1, 3, 2):
+                send(a, a(), ("xy", h, d), dev(0, x, z, yr[d]), first)
+
+    def tile_relay(h):
+        @pl.when(second)
+        def _():
+            for e in range(NS):
+                es = pl.ds(e * SUB, SUB)
+                wait(xt.at[h, ym, :, :, es], ("g", h, e, 0))
+                a = lambda es=es: xt.at[h, ym, 0:2, :, es]
+                send(a, a(), ("g", h, e, 3), dev(1, x, z, yq), second)
+                wait(xt.at[h, yq, :, :, es], ("g", h, e, 1))
+                b = lambda es=es: xt.at[h, yq, 2:4, :, es]
+                send(b, b(), ("g", h, e, 4), dev(1, x, z, ym), second)
 
     def tile_ready(h):
         tile_arrived(h)
         ones = jnp.ones((8, TILE_D), bf16)
         for g in range(4):
-            v = xt[h, :, g].reshape(128, TILE_D).astype(f32)
-            xg[h, :, g] = (v * gz).astype(bf16).reshape(4, 32, TILE_D)
+            v = xt[h, :, g].reshape(4 * R, TILE_D).astype(f32)
+            xg[h, :, g] = (v * gz).astype(bf16).reshape(4, R, TILE_D)
             sq = v * v
             hi = sq.astype(bf16)
             lo = (sq - hi.astype(f32)).astype(bf16)
             dn = (((1,), (1,)), ((), ()))
-            ssb[h, g] = lax.dot_general(
+            ssb[h, g, :, 0 : 4 * R] = lax.dot_general(
                 ones, hi, dn, preferred_element_type=f32
             ) + lax.dot_general(ones, lo, dn, preferred_element_type=f32)
         for d in (1, 3, 2):
@@ -247,15 +291,14 @@
             wait(ssr.at[h, d - 1], ("ss", h, d))
         total = ssb[h, z] + ssr[h, 0] + ssr[h, 1] + ssr[h, 2]
         scale = lax.rsqrt(total * (1.0 / D) + epsilon)
-        col = jnp.transpose(scale, (1, 0))[:, 0:1]
-        rcol[h] = jnp.broadcast_to(col, (128, 128))
+        col = jnp.transpose(scale, (1, 0))[0 : 4 * R, 0:1]
+        rcol[h] = jnp.broadcast_to(col, (4 * R, 128))
 
     def up_chunk(h, c):
         o, w = CHUNKS[c]
-        lhs = xg[h].reshape(512, TILE_D)
-        for n in range(o, o + w, 256):
-            r = jnp.dot(lhs, wu[:, n : n + 256], preferred_element_type=f32)
-            pp[h, :, :, :, n : n + 256] = r.astype(bf16).reshape(4, 4, 32, 256)
+        lhs = xg[h].reshape(16 * R, TILE_D)
+        r = jnp.dot(lhs, wu[:, o : o + w], preferred_element_type=f32)
+        pp[h, :, :, :, o : o + w] = r.astype(bf16).reshape(4, 4, R, w)
         cs = pl.ds(o, w)
         send(pp.at[h, 0:2, z2, :, cs], rz1.at[h, 0, :, :, cs], ("z1", h, c, 0), dev(p, x, zp, y))
         send(pp.at[h, 2:4, z2, :, cs], rz1.at[h, 1, :, :, cs], ("z1", h, c, 1), dev(p, x, zm, y))
@@ -289,10 +332,10 @@
             pp[h, :, z, :, cs].astype(f32)
             + rz2[h, 0, :, :, cs].astype(f32)
             + rz2[h, 1, :, :, cs].astype(f32)
-        ).reshape(128, w)
+        ).reshape(4 * R, w)
         v = s * rcol[h][:, 0:1]
         act = v / (1.0 + jnp.exp(-v))
-        ag[h, :, z, :, cs] = act.astype(bf16).reshape(4, 32, w)
+        ag[h, :, z, :, cs] = act.astype(bf16).reshape(4, R, w)
         a = ag.at[h, :, z, :, cs]
         send(a, a, ("a", h, c, 0), dev(p, x, zp, y))
         send(a, a, ("a", h, c, 1), dev(p, x, zm, y))
@@ -307,161 +350,216 @@
         b = ag.at[h, 2:4, zp, :, cs]
         send(b, b, ("a", h, c, 3), dev(p, x, zm, y))
 
-    def down_chunk(h, c):
+    def down_arrived(h, c):
+        cs = pl.ds(*CHUNKS[c])
+        wait(ag.at[h, 0:2, z2, :, cs], ("a", h, c, 2))
+        wait(ag.at[h, 2:4, z2, :, cs], ("a", h, c, 3))
+
+    def down_chunk(h, c, e=None):
         o, w = CHUNKS[c]
         cs = pl.ds(o, w)
-        wait(ag.at[h, 0:2, z2, :, cs], ("a", h, c, 2))
-        wait(ag.at[h, 2:4, z2, :, cs], ("a", h, c, 3))
-        lhs = ag[h, :, :, :, cs].reshape(512, w)
-        for n in range(0, TILE_D, 256):
+        if e is None:
+            down_arrived(h, c)
+        lhs = ag[h, :, :, :, cs].reshape(16 * R, w)
+        for n in range(0 if e is None else e * SUB, TILE_D if e is None else (e + 1) * SUB, 256):
             r = jnp.dot(lhs, wd[cs, n : n + 256], preferred_element_type=f32)
             if c > 0:
-                r = r + yacc[:, n : n + 256]
+                r = r + yacc[h, :, n : n + 256]
             if c == NC - 1:
-                yp[h, :, :, :, n : n + 256] = r.astype(bf16).reshape(4, 4, 32, 256)
+                yp[h, :, :, :, n : n + 256] = r.astype(bf16).reshape(4, 4, R, 256)
             else:
-                yacc[:, n : n + 256] = r
-
-    def y_start(h):
-        send(yp.at[h, y2, 0:2], ry1.at[h, 0], ("y1", h, 0), dev(p, x, z, yq))
-        send(yp.at[h, y2, 2:4], ry1.at[h, 1], ("y1", h, 1), dev(p, x, z, ym))
-        send(yp.at[h, yq, 2:4], ry2.at[h, 0, 2:4], ("y2", h, 0), dev(p, x, z, yq))
-        send(yp.at[h, ym, 0:2], ry2.at[h, 1, 0:2], ("y2", h, 1), dev(p, x, z, ym))
-
-    def y_mid(h):
-        wait(ry1.at[h, 0], ("y1", h, 0))
-        yp[h, yq, 0:2] = (yp[h, yq, 0:2].astype(f32) + ry1[h, 0].astype(f32)).astype(bf16)
-        send(yp.at[h, yq, 0:2], ry2.at[h, 0, 0:2], ("y2", h, 2), dev(p, x, z, yq))
-        wait(ry1.at[h, 1], ("y1", h, 1))
-        yp[h, ym, 2:4] = (yp[h, ym, 2:4].astype(f32) + ry1[h, 1].astype(f32)).astype(bf16)
-        send(yp.at[h, ym, 2:4], ry2.at[h, 1, 2:4], ("y2", h, 3), dev(p, x, z, ym))
-
-    def y_end(h):
-        wait(ry2.at[h, 0, 2:4], ("y2", h, 0))
-        wait(ry2.at[h, 1, 0:2], ("y2", h, 1))
-        wait(ry2.at[h, 0, 0:2], ("y2", h, 2))
-        wait(ry2.at[h, 1, 2:4], ("y2", h, 3))
-        sh[h] = (
-            xt[h, y].astype(f32) + yp[h, y].astype(f32) + ry2[h, 0].astype(f32) + ry2[h, 1].astype(f32)
+                yacc[h, :, n : n + 256] = r
+
+    def y_start(h, e):
+        es = pl.ds(e * SUB, SUB)
+        send(yp.at[h, y2, 0:2, :, es], ry1.at[h, 0, :, :, es], ("y1", h, e, 0), dev(p, x, z, yq))
+        send(yp.at[h, y2, 2:4, :, es], ry1.at[h, 1, :, :, es], ("y1", h, e, 1), dev(p, x, z, ym))
+        send(yp.at[h, yq, 2:4, :, es], ry2.at[h, 0, 2:4, :, es], ("y2", h, e, 0), dev(p, x, z, yq))
+        send(yp.at[h, ym, 0:2, :, es], ry2.at[h, 1, 0:2, :, es], ("y2", h, e, 1), dev(p, x, z, ym))
+
+    def y_mid(h, e):
+        es = pl.ds(e * SUB, SUB)
+        wait(ry1.at[h, 0, :, :, es], ("y1", h, e, 0))
+        yp[h, yq, 0:2, :, es] = (
+            yp[h, yq, 0:2, :, es].astype(f32) + ry1[h, 0, :, :, es].astype(f32)
         ).astype(bf16)
+        send(yp.at[h, yq, 0:2, :, es], ry2.at[h, 0, 0:2, :, es], ("y2", h, e, 2), dev(p, x, z, yq))
+        wait(ry1.at[h, 1, :, :, es], ("y1", h, e, 1))
+        yp[h, ym, 2:4, :, es] = (
+            yp[h, ym, 2:4, :, es].astype(f32) + ry1[h, 1, :, :, es].astype(f32)
+        ).astype(bf16)
+        send(yp.at[h, ym, 2:4, :, es], ry2.at[h, 1, 2:4, :, es], ("y2", h, e, 3), dev(p, x, z, ym))
+
+    def y_end(h, e):
+        es = pl.ds(e * SUB, SUB)
+        wait(ry2.at[h, 0, 2:4, :, es], ("y2", h, e, 0))
+        wait(ry2.at[h, 1, 0:2, :, es], ("y2", h, e, 1))
+        wait(ry2.at[h, 0, 0:2, :, es], ("y2", h, e, 2))
+        wait(ry2.at[h, 1, 2:4, :, es], ("y2", h, e, 3))
+        sh[h, :, :, es] = (
+            xt[h, y, :, :, es].astype(f32)
+            + yp[h, y, :, :, es].astype(f32)
+            + ry2[h, 0, :, :, es].astype(f32)
+            + ry2[h, 1, :, :, es].astype(f32)
+        ).astype(bf16)
 
         @pl.when(first)
         def _():
-            dst = xt.at[h, y]
-            send(lambda: sh.at[h], dst, ("g", h, 0), dev(1, x, z, yq), first)
-            send(lambda: sh.at[h], dst, ("g", h, 1), dev(1, x, z, ym), first)
-            send(lambda: sh.at[h], dst, ("g", h, 2), dev(1, x, z, y), first)
+            dst = xt.at[h, y, :, :, es]
+            src = lambda: sh.at[h, :, :, es]
+            send(src, dst, ("g", h, e, 0), dev(1, x, z, yq), first)
+            send(src, dst, ("g", h, e, 1), dev(1, x, z, ym), first)
+            send(src, dst, ("g", h, e, 2), dev(1, x, z, y), first)
 
         @pl.when(second)
         def _():
             for d in (1, 3, 2):
-                zt = zr[d]
-                for xb in range(4):
+                for xb in range(e * XB, (e + 1) * XB):
                     send(
                         lambda d=d, xb=xb: sh.at[h, zr[d], :, pl.ds(xb * BLK, BLK)],
                         xf.at[h, y, :, hcols(xb, 0)],
-                        ("f", h, d, xb), dev(1, x, zt, y), second,
+                        ("f", h, d, xb), dev(1, x, zr[d], y), second,
                     )
-            for xb in range(4):
+            for xb in range(e * XB, (e + 1) * XB):
                 xf[h, y, :, hcols(xb, 0)] = sh[h, z, :, xb * BLK : (xb + 1) * BLK]
 
-    half_d = D // 2
-
-    def finals_one(h):
+    FW = D // NS
+
+    def fcols(e, part=None):
+        if part is None:
+            return pl.ds(e * FW, FW)
+        return pl.ds(e * FW + part * (FW // 2), FW // 2)
+
+    def finals_one(h, e):
         @pl.when(second)
         def _():
             for d in (1, 3, 2):
-                zs = zr[(4 - d) % 4]
-                for xb in range(4):
+                for xb in range(e * XB, (e + 1) * XB):
                     wait(xf.at[h, y, :, hcols(xb, (4 - d) % 4)], ("f", h, d, xb))
-            a = lambda: xf.at[h, y]
-            send(a, a(), ("q", h, 0), dev(1, x, z, yq), second)
-            send(a, a(), ("q", h, 1), dev(1, x, z, ym), second)
-            send(a, a(), ("q", h, 4), dev(0, x, z, y), second)
-
-    def finals_two(h):
+            a = lambda: xf.at[h, y, :, fcols(e)]
+            send(a, a(), ("q", h, e, 0), dev(1, x, z, yq), second)
+            send(a, a(), ("q", h, e, 1), dev(1, x, z, ym), second)
+            send(a, a(), ("q", h, e, 4), dev(0, x, z, y), second)
+
+    def finals_two(h, e):
         @pl.when(second)
         def _():
-            wait(xf.at[h, ym], ("q", h, 0))
-            a = lambda: xf.at[h, ym, :, pl.ds(0, half_d)]
-            send(a, a(), ("q", h, 2), dev(1, x, z, yq), second)
-            wait(xf.at[h, yq], ("q", h, 1))
-            b = lambda: xf.at[h, yq, :, pl.ds(half_d, half_d)]
-            send(b, b(), ("q", h, 3), dev(1, x, z, ym), second)
-            e = lambda: xf.at[h, ym]
-            send(e, e(), ("q", h, 5), dev(0, x, z, y), second)
-            f = lambda: xf.at[h, yq]
-            send(f, f(), ("q", h, 6), dev(0, x, z, y), second)
-
-    def finals_three(h):
+            wait(xf.at[h, ym, :, fcols(e)], ("q", h, e, 0))
+            a = lambda: xf.at[h, ym, :, fcols(e, 0)]
+            send(a, a(), ("q", h, e, 2), dev(1, x, z, yq), second)
+            wait(xf.at[h, yq, :, fcols(e)], ("q", h, e, 1))
+            b = lambda: xf.at[h, yq, :, fcols(e, 1)]
+            send(b, b(), ("q", h, e, 3), dev(1, x, z, ym), second)
+            a2 = lambda: xf.at[h, ym, :, fcols(e)]
+            send(a2, a2(), ("q", h, e, 5), dev(0, x, z, y), second)
+            b2 = lambda: xf.at[h, yq, :, fcols(e)]
+            send(b2, b2(), ("q", h, e, 6), dev(0, x, z, y), second)
+
+    def finals_three(h, e):
         @pl.when(second)
         def _():
-            wait(xf.at[h, y2, :, pl.ds(0, half_d)], ("q", h, 2))
-            wait(xf.at[h, y2, :, pl.ds(half_d, half_d)], ("q", h, 3))
-            a = lambda: xf.at[h, y2]
-            send(a, a(), ("q", h, 7), dev(0, x, z, y), second)
-
+            wait(xf.at[h, y2, :, fcols(e, 0)], ("q", h, e, 2))
+            wait(xf.at[h, y2, :, fcols(e, 1)], ("q", h, e, 3))
+            a = lambda: xf.at[h, y2, :, fcols(e)]
+            send(a, a(), ("q", h, e, 7), dev(0, x, z, y), second)
+
+    def finals_here(h):
         @pl.when(first)
         def _():
-            wait(xf.at[h, y], ("q", h, 4))
-            wait(xf.at[h, ym], ("q", h, 5))
-            wait(xf.at[h, yq], ("q", h, 6))
-            wait(xf.at[h, y2], ("q", h, 7))
-
-    def final_norm(h):
-        for q in range(4):
-            v = xf[h, q].astype(f32)
-            r = lax.rsqrt(jnp.mean(v * v, axis=1, keepdims=True) + epsilon)
-            xn[pl.ds(h * 128 + q * 32, 32), :] = (v * r * fgain[...]).astype(bf16)
-
-    steps = [(h, c) for h in range(NH) for c in range(NC)]
-    lw.wait()
-    ld.wait()
-
-    def y_tail(h, stage):
-        if stage == 0:
-            y_start(h)
-        elif stage == 1:
-            y_mid(h)
+            for e in range(NS):
+                wait(xf.at[h, y, :, fcols(e)], ("q", h, e, 4))
+                wait(xf.at[h, ym, :, fcols(e)], ("q", h, e, 5))
+                wait(xf.at[h, yq, :, fcols(e)], ("q", h, e, 6))
+                wait(xf.at[h, y2, :, fcols(e)], ("q", h, e, 7))
+
+    def final_norm(h, cond):
+        def work():
+            for q in range(4):
+                v = xf[h, q].astype(f32)
+                r = lax.rsqrt(jnp.mean(v * v, axis=1, keepdims=True) + epsilon)
+                xn[pl.ds((h * 4 + q) * R, R), :] = (v * r * fgain[...]).astype(bf16)
+
+        if cond is None:
+            work()
         else:
-            y_end(h)
+            pl.when(cond)(work)
+
+    steps = [(h, c) for c in range(NC) for h in range(2)]
+    steps += [(h, c) for h in range(2, NH) for c in range(NC)]
+    with jax.named_scope("local_weights"):
+        ld.start()
+        lw.wait()
 
     n = len(steps)
-    y_events = {}
-    for i in range(n + NC + 8):
-        if i < len(items):
-            weights_forward(i)
-        if i - 1 >= 0 and i - 1 < n:
-            reduce_one(*steps[i - 1])
-        if i - 2 >= 0 and i - 2 < n:
-            reduce_two(*steps[i - 2])
-        if i - 3 >= 0 and i - 3 < n:
-            gather_one(*steps[i - 3])
-        if i < n:
-            h, c = steps[i]
-            if h == 0:
-                weights_last(i)
-            if c == 0:
-                tile_ready(h)
-            up_chunk(h, c)
-        j = i - NC - 1
-        if 0 <= j < n:
-            h, c = steps[j]
-            if h == 0:
-                weights_last(NC + c)
-            down_chunk(h, c)
-            if c == NC - 1:
-                y_start(h)
-                y_events.setdefault(i + 1, []).append((y_mid, h))
-                y_events.setdefault(i + 2, []).append((y_end, h))
-                y_events.setdefault(i + 3, []).append((finals_one, h))
-        for f, h in y_events.pop(i, []):
-            f(h)
-    assert not y_events
+    slots = {}
+
+    def prefetch(a, b):
+        for k in range(a, b):
+            ucopy(k).start()
+
+
+    def at(slot, prio, fn, *args):
+        slots.setdefault(slot, []).append((prio, len(slots[slot]) if slot in slots else 0, fn, args))
+
+    for k in range(PRE):
+        at(-1, 0, weights_forward, k, second)
+    at(-1, 1, tile_relay_first, 0)
+    at(-1, 1, tile_relay_first, 1)
+    at(3, 8, ld.wait)
+    at(3, 9, prefetch, 0, NSLOT)
+    at(-1, 1, tile_relay, 0)
+    at(1, 9, tile_relay, 1)
+    for h in range(2, NH):
+        at(h, 3, near_later, h)
+        at(h + 2, 3, tile_relay_first, h)
+        at(steps.index((h, 0)) - 1, 9, tile_relay, h)
+    for k in range(2 * NC):
+        at(WF_SLOT[k], 0 if k == 0 else 2, weights_forward, k, first)
+    for k in range(PRE, 2 * NC):
+        at(1 + 2 * (k - PRE), 2, weights_forward, k, second)
+    last = {}
+    for i, (h, c) in enumerate(steps):
+        u = i + 1
+        if h == 0:
+            at(u, 2, weights_last, c)
+        if c == 0:
+            at(u, 2, tile_ready, h)
+        at(u, 2, up_chunk, h, c)
+        at(u + LAG, 3, reduce_one, h, c)
+        at(u + 2 * LAG, 4, reduce_two, h, c)
+        at(u + 3 * LAG, 5, gather_one, h, c)
+        slot = max(u + 4 * LAG, WF_SLOT[NC + c] + 2 + h)
+        if h == 0:
+            at(slot, 6, weights_last, NC + c)
+        if c < NC - 1 or NS == 1:
+            at(slot, 6, down_chunk, h, c)
+        else:
+            at(slot, 6, down_arrived, h, c)
+        if c == NC - 1:
+            for e in range(NS):
+                if NS > 1:
+                    at(slot, 7, down_chunk, h, c, e)
+                at(slot, 7, y_start, h, e)
+        last[h] = slot
     for h in range(NH):
-        finals_two(h)
-        finals_three(h)
-        final_norm(h)
+        slot = last[h]
+        lags = (1, 2, 4, 6, 7) if h < NH - 1 else (1, 2, 3, 4, 5)
+        for e in range(NS):
+            for lag, fn in zip(lags, (y_mid, y_end, finals_one, finals_two, finals_three)):
+                at(slot + lag, 8, fn, h, e)
+        if h < NH - 1:
+            at(slot + 8, 13, final_norm, h, second)
+    end = max(slots) + 1
+    for h in range(NH):
+        at(end, h, finals_here, h)
+        if h < NH - 1:
+            at(end, h, final_norm, h, first)
+        else:
+            at(end, h, final_norm, h, None)
+    for slot in sorted(slots):
+        for _, _, fn, args in sorted(slots[slot], key=lambda e: e[:2]):
+            with jax.named_scope(getattr(fn, "__name__", "copy")):
+                fn(*args)
 
     for d in (1, 2, 3):
         wait(cx.at[xr[(4 - d) % 4]], ("cx", d))
@@ -497,7 +595,8 @@
 
         return carry
 
-    lax.fori_loop(0, NU, head, 0)
+    with jax.named_scope("head"):
+        lax.fori_loop(0, NU, head, 0)
 
     st[vocab_index, 0:8] = m_s[...]
     st[vocab_index, 8:16] = s_s[...]
@@ -508,11 +607,14 @@
         if d > 0:
             send(mine, mine, ("st", 0, d), dev(p, x, z, yt))
         send(mine, mine, ("st", 1, d), dev(other, x, z, yt))
+    stat = jax.named_scope("stats_wait")
+    stat.__enter__()
     for d in range(4):
         ys = yr[(4 - d) % 4]
         if d > 0:
             wait(st.at[p * 4 + ys], ("st", 0, d))
         wait(st.at[other * 4 + ys], ("st", 1, d))
+    stat.__exit__(None, None, None)
     ms = [st[i, 0:8] for i in range(8)]
     top = ms[0]
     for i in range(1, 8):
@@ -555,23 +657,23 @@
         scratch_shapes=[
             V((TILE_D, FF_DEV), bf16),
             V((FF_DEV, TILE_D), bf16),
-            V((NH, 4, 4, 32, TILE_D), bf16),
-            V((NH, 4, 4, 32, TILE_D), bf16),
-            V((NH, 4, 4, 32, FF_DEV), bf16),
-            V((NH, 2, 2, 32, FF_DEV), bf16),
-            V((NH, 2, 4, 32, FF_DEV), bf16),
-            V((NH, 4, 4, 32, FF_DEV), bf16),
-            V((512, TILE_D), f32),
-            V((NH, 4, 4, 32, TILE_D), bf16),
-            V((NH, 2, 2, 32, TILE_D), bf16),
-            V((NH, 2, 4, 32, TILE_D), bf16),
-            V((NH, 4, 32, TILE_D), bf16),
-            V((NH, 4, 32, D), bf16),
+            V((NH, 4, 4, R, TILE_D), bf16),
+            V((NH, 4, 4, R, TILE_D), bf16),
+            V((NH, 4, 4, R, FF_DEV), bf16),
+            V((NH, 2, 2, R, FF_DEV), bf16),
+            V((NH, 2, 4, R, FF_DEV), bf16),
+            V((NH, 4, 4, R, FF_DEV), bf16),
+            V((NH, 16 * R, TILE_D), f32),
+            V((NH, 4, 4, R, TILE_D), bf16),
+            V((NH, 2, 2, R, TILE_D), bf16),
+            V((NH, 2, 4, R, TILE_D), bf16),
+            V((NH, 4, R, TILE_D), bf16),
+            V((NH, 4, R, D), bf16),
             V((256, D), bf16),
             V((NSLOT, UROWS, D), bf16),
             V((NH, 4, 8, 128), f32),
             V((NH, 3, 8, 128), f32),
-            V((NH, 128, 128), f32),
+            V((NH, 4 * R, 128), f32),
             V((8, 24, 256), f32),
             V((4, 8, 128), f32),
             V((4, 8, 128), f32),
@@ -594,7 +696,7 @@
     target_ids, response_masks, anchor_logps, pairing,
 ):
     tok, cnt = run(
-        hidden_states.reshape(NH, 4, 32, D),
+        hidden_states.reshape(NH, 4, R, D),
         up_weight[0],
         down_weight[0],
         layer_gain,

time: 192 us -> 164 us (0.85)
  Pallas kernels: 186 us -> 159 us
    pallas_call x1, Pallas kernels: 186 us -> 159 us  [run(): pl.pallas_call(body, out_shape=(jax.ShapeDtypeStruct((8, 256), f32), jax....]
where the time goes in v2:
time: 164 us
  Pallas kernels  159 us (97%)
  local copies, waits for them, and re-layouts  2.34 us (1%)
  other arithmetic  2.2 us (1%)
    pallas_call x1, Pallas kernels, run(): pl.pallas_call(body, out_shape=(jax.ShapeDtypeStruct((8, 256), f32), jax....  159 us

profile of v2, /device:TPU:1, one launch (start us, length us, event | category | flops | bytes accessed | tf_op | source)
XLA Modules:
  0.0 163.7 jit_solution(13759116765460407792)
XLA Ops:
  0.6 0.0 copy-start
  0.6 0.0 copy-start.2
  0.7 0.0 copy-start.3
  0.7 1.3 reshape.33.ids
  2.0 158.5 %relay.1 = (f32[8,256]{1,0:T(8,128)}, f32[8,128]{1,0:T(8,128)}) custom-call(bf16[4,4,16,4096]{3,2,1,0:T(8,128)(2,1)} %bitcast.6, bf16[256,1792]{1,0:T(8,128)(2,1)} %bitcast.7, bf16[1792,256]{1,0:T(8,128)(2,1)} %bitcast.8, f32[1,4096]{1,0:T(1,128)} %lgain.1, f32[1,4096]{1,0:T(1,128)} %bitcast.9, bf16[4096,4096]{1,0:T(8,128)(2,1)} %unemb.1, ...), custom_call_target="tpu_custom_call" | custom-call | tf_op jit(solution)/shard_map/relay/pallas_call | solution.py:649
  160.5 0.7 slice_reduce_fusion
  161.2 0.1 reshape_squeeze.3
  161.3 0.0 copy-done
  161.3 0.0 copy-done.2
  161.3 0.0 copy-start.1
  161.3 0.1 multiply_reduce_fusion
  161.5 0.8 multiply_reduce_fusion.1
  162.3 0.5 divide_subtract_fusion
  162.8 0.0 copy-done.3
  162.8 0.1 slice.14
  162.9 0.1 slice.15
  163.0 0.2 fusion.1
  163.2 0.5 add_multiply_fusion
  163.7 0.0 copy-done.1
Async XLA Ops:
  0.6 160.7 %copy-start = (s32[4,64]{1,0:T(4,128)S(1)}, s32[4,64]{1,0:T(4,128)}, u32[]{:S(2)}) copy-start(s32[4,64]{1,0:T(4,128)} %mask.1) | copy-start | bytes 3076
  0.6 160.7 %copy-start.2 = (f32[4,64]{1,0:T(4,128)S(1)}, f32[4,64]{1,0:T(4,128)}, u32[]{:S(2)}) copy-start(f32[4,64]{1,0:T(4,128)} %param.18) | copy-start | bytes 3076
  0.7 162.2 %copy-start.3 = (s32[1,4]{1,0:T(1,128)S(1)}, s32[1,4]{1,0:T(1,128)}, u32[]{:S(2)}) copy-start(s32[1,4]{1,0:T(1,128)} %param.19) | copy-start | bytes 52
  161.3 2.4 %copy-start.1 = (f32[4,64]{1,0:T(4,128)}, f32[4,64]{1,0:T(4,128)S(1)}, u32[]{:S(2)}) copy-start(f32[4,64]{1,0:T(4,128)S(1)} %reshape_squeeze.3) | copy-start | bytes 3076

commit v3 on v2

--- a/solution.py
+++ b/solution.py
@@ -16,14 +16,17 @@
 NH = 4
 R = 32 // (NH // 2)
 AHEAD = 2
+END = ((2, 3, 4, 6), (1, 2, 3, 4))
+LAGS = ((2, 4, 6, 7, 8), (2, 4, 5, 6, 7), (2, 3, 4, 5, 6), (1, 2, 3, 4, 5))
+ORDER = (8, 8.1, 8.3, 8.2)
 WF_SLOT = (-1, 0, 2, 4, 6, 8, 10, 12)
 GATE = 0
 PRE = 4
 CHUNKS = ((0, 256), (256, 512), (768, 512), (1280, 512))
 LAG = 2
 NC = len(CHUNKS)
-UROWS = 512
-NSLOT = 6
+UROWS = 1024
+NSLOT = 3
 V_DEV = 4096
 NU = V_DEV // UROWS
 NS = 1
@@ -36,8 +39,8 @@
 
 
 def body(
-    hs, up, down, lgain, fgain, unemb, ids, mask,
-    o_tok, o_cnt,
+    hs, up, down, lgain, fgain, unemb, ids, mask, anchor, pairing,
+    out,
     wu, wd, xt, xg, pp, rz1, rz2, ag, yacc, yp, ry1, ry2, sh, xf, xn, ub,
     ssb, ssr, rcol, st, cx, cz, m_s, s_s, k_s,
     sems, usem, gate,
@@ -67,6 +70,13 @@
         return sems.at[names[key]]
 
     pending = []
+    recorded = set()
+    turn = [None]
+
+    def when(core):
+        if turn[0] is None:
+            return pl.when(core)
+        return (lambda fn: fn()) if turn[0] is core else (lambda fn: None)
 
     def send(src, dst, key, to, cond=None):
         cp = pltpu.make_async_remote_copy(
@@ -74,7 +84,9 @@
             device_id=to, device_id_type=pl.DeviceIdType.MESH,
         )
         cp.start()
-        pending.append((src, ("s", key), cond))
+        if (key, id(cond)) not in recorded:
+            recorded.add((key, id(cond)))
+            pending.append((src, ("s", key), cond))
 
     def wait(dst, key):
         pltpu.make_async_copy(dst, dst, sem(("r", key))).wait()
@@ -107,6 +119,7 @@
 
     cx[...] = jnp.zeros_like(cx)
     cz[...] = jnp.zeros_like(cz)
+    st[...] = jnp.zeros_like(st)
     ssb[...] = jnp.zeros_like(ssb)
 
     bar = pltpu.get_barrier_semaphore()
@@ -178,9 +191,10 @@
 
     def far_tokens(h):
         for xb in range(4):
+            part = slice(None) if h == 0 else y
             send(
-                lambda h=h, xb=xb: hs.at[h, y, :, hcols(xb, 2)],
-                xt.at[h, y, z, :, pl.ds(xb * BLK, BLK)],
+                lambda h=h, xb=xb, part=part: hs.at[h, part, :, hcols(xb, 2)],
+                xt.at[h, part, z, :, pl.ds(xb * BLK, BLK)],
                 ("x", h, 2, xb), dev(0, x, z2, y), first,
             )
 
@@ -207,10 +221,10 @@
     def _():
         weights_own(0, first)
         weights_own(1, first)
-        for h in range(NH):
+        far_tokens(0)
+        near_tokens(0)
+        for h in range(1, NH):
             far_tokens(h)
-            if h < 2:
-                near_tokens(h)
 
     own = jnp.sum(mask[...].astype(f32), axis=1, keepdims=True)
     cx[x, 0:4, :] = jnp.broadcast_to(own, (4, 128))
@@ -237,8 +251,12 @@
                 zs = zr[(4 - d) % 4]
                 for xb in range(4):
                     wait(xt.at[h, :, zs, :, pl.ds(xb * BLK, BLK)], ("x", h, d, xb))
-            for d in (1, 3, 2):
-                wait(xt.at[h, yr[(4 - d) % 4], z2], ("xy", h, d))
+            if h == 0:
+                for xb in range(4):
+                    wait(xt.at[h, :, z2, :, pl.ds(xb * BLK, BLK)], ("x", h, 2, xb))
+            else:
+                for d in (1, 3, 2):
+                    wait(xt.at[h, yr[(4 - d) % 4], z2], ("xy", h, d))
 
         @pl.when(second)
         def _():
@@ -383,12 +401,12 @@
         yp[h, yq, 0:2, :, es] = (
             yp[h, yq, 0:2, :, es].astype(f32) + ry1[h, 0, :, :, es].astype(f32)
         ).astype(bf16)
-        send(yp.at[h, yq, 0:2, :, es], ry2.at[h, 0, 0:2, :, es], ("y2", h, e, 2), dev(p, x, z, yq))
+        send(lambda: yp.at[h, yq, 0:2, :, es], ry2.at[h, 0, 0:2, :, es], ("y2", h, e, 2), dev(p, x, z, yq))
         wait(ry1.at[h, 1, :, :, es], ("y1", h, e, 1))
         yp[h, ym, 2:4, :, es] = (
             yp[h, ym, 2:4, :, es].astype(f32) + ry1[h, 1, :, :, es].astype(f32)
         ).astype(bf16)
-        send(yp.at[h, ym, 2:4, :, es], ry2.at[h, 1, 2:4, :, es], ("y2", h, e, 3), dev(p, x, z, ym))
+        send(lambda: yp.at[h, ym, 2:4, :, es], ry2.at[h, 1, 2:4, :, es], ("y2", h, e, 3), dev(p, x, z, ym))
 
     def y_end(h, e):
         es = pl.ds(e * SUB, SUB)
@@ -403,7 +421,7 @@
             + ry2[h, 1, :, :, es].astype(f32)
         ).astype(bf16)
 
-        @pl.when(first)
+        @when(first)
         def _():
             dst = xt.at[h, y, :, :, es]
             src = lambda: sh.at[h, :, :, es]
@@ -411,7 +429,7 @@
             send(src, dst, ("g", h, e, 1), dev(1, x, z, ym), first)
             send(src, dst, ("g", h, e, 2), dev(1, x, z, y), first)
 
-        @pl.when(second)
+        @when(second)
         def _():
             for d in (1, 3, 2):
                 for xb in range(e * XB, (e + 1) * XB):
@@ -431,7 +449,7 @@
         return pl.ds(e * FW + part * (FW // 2), FW // 2)
 
     def finals_one(h, e):
-        @pl.when(second)
+        @when(second)
         def _():
             for d in (1, 3, 2):
                 for xb in range(e * XB, (e + 1) * XB):
@@ -442,7 +460,7 @@
             send(a, a(), ("q", h, e, 4), dev(0, x, z, y), second)
 
     def finals_two(h, e):
-        @pl.when(second)
+        @when(second)
         def _():
             wait(xf.at[h, ym, :, fcols(e)], ("q", h, e, 0))
             a = lambda: xf.at[h, ym, :, fcols(e, 0)]
@@ -456,7 +474,7 @@
             send(b2, b2(), ("q", h, e, 6), dev(0, x, z, y), second)
 
     def finals_three(h, e):
-        @pl.when(second)
+        @when(second)
         def _():
             wait(xf.at[h, y2, :, fcols(e, 0)], ("q", h, e, 2))
             wait(xf.at[h, y2, :, fcols(e, 1)], ("q", h, e, 3))
@@ -499,12 +517,17 @@
 
 
     def at(slot, prio, fn, *args):
-        slots.setdefault(slot, []).append((prio, len(slots[slot]) if slot in slots else 0, fn, args))
+        entry = (prio, len(slots.get(slot, ())), fn, args, None)
+        slots.setdefault(slot, []).append(entry)
+
+    def at_core(core, slot, prio, fn, *args):
+        entry = (prio, len(slots.get(slot, ())), fn, args, core)
+        slots.setdefault(slot, []).append(entry)
 
     for k in range(PRE):
         at(-1, 0, weights_forward, k, second)
-    at(-1, 1, tile_relay_first, 0)
-    at(-1, 1, tile_relay_first, 1)
+    at(-1, 1, near_later, 1)
+    at(0, 1, tile_relay_first, 1)
     at(3, 8, ld.wait)
     at(3, 9, prefetch, 0, NSLOT)
     at(-1, 1, tile_relay, 0)
@@ -525,10 +548,15 @@
         if c == 0:
             at(u, 2, tile_ready, h)
         at(u, 2, up_chunk, h, c)
-        at(u + LAG, 3, reduce_one, h, c)
-        at(u + 2 * LAG, 4, reduce_two, h, c)
-        at(u + 3 * LAG, 5, gather_one, h, c)
-        slot = max(u + 4 * LAG, WF_SLOT[NC + c] + 2 + h)
+        stage = [u + k * LAG for k in range(1, 5)]
+        if h >= NH - 2:
+            end = steps.index((h, NC - 1)) + 1
+            cap = END[h - NH + 2]
+            stage = [min(t, end + d) for t, d in zip(stage, cap)]
+        at(stage[0], 3, reduce_one, h, c)
+        at(stage[1], 4, reduce_two, h, c)
+        at(stage[2], 5, gather_one, h, c)
+        slot = max(stage[3], WF_SLOT[NC + c] + 2 + h)
         if h == 0:
             at(slot, 6, weights_last, NC + c)
         if c < NC - 1 or NS == 1:
@@ -543,12 +571,13 @@
         last[h] = slot
     for h in range(NH):
         slot = last[h]
-        lags = (1, 2, 4, 6, 7) if h < NH - 1 else (1, 2, 3, 4, 5)
-        for e in range(NS):
-            for lag, fn in zip(lags, (y_mid, y_end, finals_one, finals_two, finals_three)):
-                at(slot + lag, 8, fn, h, e)
+        at_core(first, slot + 1, 8, y_mid, h, 0)
+        at_core(first, slot + 2, 8, y_end, h, 0)
+        fns = (y_mid, y_end, finals_one, finals_two, finals_three)
+        for lag, fn in zip(LAGS[h], fns):
+            at_core(second, slot + lag, ORDER[h], fn, h, 0)
         if h < NH - 1:
-            at(slot + 8, 13, final_norm, h, second)
+            at(slot + LAGS[h][-1], 13, final_norm, h, second)
     end = max(slots) + 1
     for h in range(NH):
         at(end, h, finals_here, h)
@@ -557,9 +586,14 @@
         else:
             at(end, h, final_norm, h, None)
     for slot in sorted(slots):
-        for _, _, fn, args in sorted(slots[slot], key=lambda e: e[:2]):
+        for _, _, fn, args, core in sorted(slots[slot], key=lambda e: e[:2]):
             with jax.named_scope(getattr(fn, "__name__", "copy")):
-                fn(*args)
+                if core is None:
+                    fn(*args)
+                else:
+                    turn[0] = core
+                    pl.when(core)(lambda: fn(*args))
+                    turn[0] = None
 
     for d in (1, 2, 3):
         wait(cx.at[xr[(4 - d) % 4]], ("cx", d))
@@ -567,10 +601,25 @@
     for d in (1, 2, 3):
         send(cz.at[z], cz.at[z], ("cz", d), dev(p, x, zr[d], y))
 
+    vocab_index = p * 4 + y
+    lanes = lax.broadcasted_iota(jnp.int32, (64, 256), 1)
+    spread = (lanes % 64 == lax.broadcasted_iota(jnp.int32, (64, 256), 0)).astype(bf16)
+    own_row = lax.broadcasted_iota(jnp.int32, (8, 256), 1) // 64 == lax.broadcasted_iota(
+        jnp.int32, (8, 256), 0
+    )
+
+    def to_row(v):
+        r = jnp.dot(v, spread, preferred_element_type=f32)
+        return jnp.sum(jnp.where(own_row, r, 0.0), axis=0, keepdims=True)
+
+    idp = jnp.concatenate([ids[...], jnp.zeros((4, 64), jnp.int32)], axis=0)
+    high = to_row((idp // 256).astype(f32).astype(bf16))
+    low = to_row((idp % 256).astype(f32).astype(bf16))
+    id_row = (high * 256.0 + low).astype(jnp.int32) - vocab_index * V_DEV
+
     m_s[...] = jnp.full_like(m_s, -jnp.inf)
     s_s[...] = jnp.zeros_like(s_s)
     k_s[...] = jnp.zeros_like(k_s)
-    vocab_index = p * 4 + y
 
     def head(k, carry):
         slot = lax.rem(k, NSLOT)
@@ -578,16 +627,14 @@
         lt = lax.dot_general(
             ub[slot], xn[...], (((1,), (1,)), ((), ())), preferred_element_type=f32
         )
-        m_old = m_s[0:1, :]
+        m_old = m_s[...]
         m_new = jnp.maximum(m_old, jnp.max(lt, axis=0, keepdims=True))
-        rows = lax.broadcasted_iota(jnp.int32, lt.shape, 0) + (vocab_index * V_DEV + k * UROWS)
-        k_s[0:1, :] = k_s[0:1, :] + jnp.sum(
-            jnp.where(rows == ids[...], lt, 0.0), axis=0, keepdims=True
-        )
-        s_s[0:1, :] = s_s[0:1, :] * jnp.exp(m_old - m_new) + jnp.sum(
+        rows = lax.broadcasted_iota(jnp.int32, lt.shape, 0) + k * UROWS
+        k_s[...] = k_s[...] + jnp.sum(jnp.where(rows == id_row, lt, 0.0), axis=0, keepdims=True)
+        s_s[...] = s_s[...] * jnp.exp(m_old - m_new) + jnp.sum(
             jnp.exp(lt - m_new), axis=0, keepdims=True
         )
-        m_s[0:1, :] = m_new
+        m_s[...] = m_new
 
         @pl.when(k + NSLOT < NU)
         def _():
@@ -598,9 +645,9 @@
     with jax.named_scope("head"):
         lax.fori_loop(0, NU, head, 0)
 
-    st[vocab_index, 0:8] = m_s[...]
-    st[vocab_index, 8:16] = s_s[...]
-    st[vocab_index, 16:24] = k_s[...]
+    st[vocab_index, 0:1] = m_s[...]
+    st[vocab_index, 1:2] = s_s[...]
+    st[vocab_index, 2:3] = k_s[...]
     mine = st.at[vocab_index]
     for d in range(4):
         yt = yr[d]
@@ -615,24 +662,39 @@
             wait(st.at[p * 4 + ys], ("st", 0, d))
         wait(st.at[other * 4 + ys], ("st", 1, d))
     stat.__exit__(None, None, None)
-    ms = [st[i, 0:8] for i in range(8)]
+    ms = [st[i, 0:1] for i in range(8)]
     top = ms[0]
     for i in range(1, 8):
         top = jnp.maximum(top, ms[i])
     tot = jnp.zeros_like(top)
     pick = jnp.zeros_like(top)
     for i in range(8):
-        tot = tot + st[i, 8:16] * jnp.exp(ms[i] - top)
-        pick = pick + st[i, 16:24]
-    o_tok[...] = pick - top - jnp.log(tot)
-
+        tot = tot + st[i, 1:2] * jnp.exp(ms[i] - top)
+        pick = pick + st[i, 2:3]
+    row = pick - top - jnp.log(tot)
     for d in (1, 2, 3):
         wait(cz.at[zr[(4 - d) % 4]], ("cz", d))
-    o_cnt[...] = cz[0] + cz[1] + cz[2] + cz[3]
+    counts = (cz[0] + cz[1] + cz[2] + cz[3])[0:4, 0:1]
+    divisor = counts / 16.0
+    mv = mask[...].astype(f32)
+    tok = jnp.concatenate([row[:, 64 * i : 64 * i + 64] for i in range(4)], axis=0)
+    policy = jnp.sum(mv * tok, axis=1, keepdims=True) / divisor
+    gaps = policy - jnp.sum(mv * anchor[...], axis=1, keepdims=True) / divisor
+    place = lax.broadcasted_iota(jnp.int32, (4, 1), 0)
+    side = lax.broadcasted_iota(jnp.int32, (4, 64), 1)
+    extra = jnp.broadcast_to(policy, (4, 64))
+    for i in range(2):
+        chosen = jnp.sum(jnp.where(place == pairing[0, 2 * i], gaps, 0.0))
+        rejected = jnp.sum(jnp.where(place == pairing[0, 2 * i + 1], gaps, 0.0))
+        diff = chosen - rejected - 0.5 / ipo_tau
+        extra = jnp.where(side == i + 1, diff * diff, extra)
+    out[0:4, :] = jnp.concatenate([tok, extra], axis=1)
+    out[4:8, :] = jnp.zeros((4, 128), f32)
 
     for src, ssem, cond in pending:
         if cond is None:
-            pltpu.make_async_copy(src, src, sem(ssem)).wait()
+            ref = src() if callable(src) else src
+            pltpu.make_async_copy(ref, ref, sem(ssem)).wait()
     for which in (first, second):
         @pl.when(which)
         def _():
@@ -642,18 +704,18 @@
                     pltpu.make_async_copy(ref, ref, sem(ssem)).wait()
 
 
-def run(hs, up, down, lgain, fgain, unemb, ids, mask):
+def run(hs, up, down, lgain, fgain, unemb, ids, mask, anchor, pairing):
     anyspace = pl.BlockSpec(memory_space=pltpu.HBM)
     vm = pl.BlockSpec(memory_space=pltpu.VMEM)
+    sm = pl.BlockSpec(memory_space=pltpu.SMEM)
     V = pltpu.VMEM
     return pl.pallas_call(
         body,
         out_shape=(
-            jax.ShapeDtypeStruct((8, 256), f32),
-            jax.ShapeDtypeStruct((8, 128), f32),
+            jax.ShapeDtypeStruct((8, 128), f32)
         ),
-        in_specs=[anyspace, anyspace, anyspace, vm, vm, anyspace, vm, vm],
-        out_specs=(vm, vm),
+        in_specs=[anyspace, anyspace, anyspace, vm, vm, anyspace, vm, vm, vm, sm],
+        out_specs=vm,
         scratch_shapes=[
             V((TILE_D, FF_DEV), bf16),
             V((FF_DEV, TILE_D), bf16),
@@ -674,12 +736,12 @@
             V((NH, 4, 8, 128), f32),
             V((NH, 3, 8, 128), f32),
             V((NH, 4 * R, 128), f32),
-            V((8, 24, 256), f32),
+            V((8, 8, 256), f32),
             V((4, 8, 128), f32),
             V((4, 8, 128), f32),
-            V((8, 256), f32),
-            V((8, 256), f32),
-            V((8, 256), f32),
+            V((1, 256), f32),
+            V((1, 256), f32),
+            V((1, 256), f32),
             pltpu.SemaphoreType.DMA((NSEM,)),
             pltpu.SemaphoreType.DMA((NSLOT,)),
             pltpu.SemaphoreType.REGULAR,
@@ -688,39 +750,46 @@
             collective_id=0, has_side_effects=True, vmem_limit_bytes=66_000_000
         ),
         name="relay",
-    )(hs, up, down, lgain, fgain, unemb, ids, mask)
+    )(hs, up, down, lgain, fgain, unemb, ids, mask, anchor, pairing)
+
+
+def unpack(rows, tok, policy, losses):
+    tok[...] = rows[0:4, 0:64]
+    for i in range(4):
+        policy[i] = rows[i, 64]
+    for i in range(2):
+        losses[i] = rows[0, 65 + i]
 
 
 def shards(
     hidden_states, up_weight, down_weight, layer_gain, final_gain, unembedding,
     target_ids, response_masks, anchor_logps, pairing,
 ):
-    tok, cnt = run(
+    out = run(
         hidden_states.reshape(NH, 4, R, D),
         up_weight[0],
         down_weight[0],
         layer_gain,
         final_gain.reshape(1, D),
         unembedding,
-        target_ids.reshape(1, 256),
+        target_ids,
         response_masks,
+        anchor_logps,
+        pairing,
     )
-    token_logps = tok[0].reshape(4, 64)
-    counts = cnt[0:4, 0]
-    mask_values = response_masks.astype(f32)
-    divisor = counts / 16.0
-    policy = jnp.sum(mask_values * token_logps, axis=1) / divisor
-    anchor = jnp.sum(mask_values * anchor_logps, axis=1) / divisor
-    log_gaps = policy - anchor
-    positions = jnp.arange(4, dtype=jnp.int32)
-    chosen = jnp.sum(
-        jnp.where(pairing[0, 0::2][:, None] == positions[None, :], log_gaps[None, :], 0.0), axis=1
-    )
-    rejected = jnp.sum(
-        jnp.where(pairing[0, 1::2][:, None] == positions[None, :], log_gaps[None, :], 0.0), axis=1
-    )
-    losses = (chosen - rejected - 0.5 / ipo_tau) ** 2
-    return (token_logps, policy, losses)
+    vm = pl.BlockSpec(memory_space=pltpu.VMEM)
+    sm = pl.BlockSpec(memory_space=pltpu.SMEM)
+    return pl.pallas_call(
+        unpack,
+        out_shape=(
+            jax.ShapeDtypeStruct((4, 64), f32),
+            jax.ShapeDtypeStruct((4,), f32),
+            jax.ShapeDtypeStruct((2,), f32),
+        ),
+        in_specs=[vm],
+        out_specs=(vm, sm, sm),
+        name="unpack",
+    )(out)
 
 
 def solution(mesh):

time: 164 us -> 157 us (0.957)
  Pallas kernels: 159 us -> 156 us
  local copies, waits for them, and re-layouts: 2.34 us -> 0 us
  other arithmetic: 2.2 us -> 0 us
    pallas_call x1 -> x2, Pallas kernels: 159 us -> 156 us  [the longest x1 155 us: run(): pl.pallas_call(body, out_shape=jax.ShapeDtypeStruct((8, 128), f32), in_sp...]
where the time goes in v3:
time: 157 us
  Pallas kernels  156 us (99%)
    pallas_call x1, Pallas kernels, run(): pl.pallas_call(body, out_shape=jax.ShapeDtypeStruct((8, 128), f32), in_sp...  155 us

profile of v3, /device:TPU:1, one launch (start us, length us, event | category | flops | bytes accessed | tf_op | source)
XLA Modules:
  0.0 156.6 jit_solution(16226481813695069787)
XLA Ops:
  0.6 154.5 %relay.1.rows = f32[8,128]{1,0:T(8,128)} custom-call(bf16[4,4,16,4096]{3,2,1,0:T(8,128)(2,1)} %bitcast.4, bf16[256,1792]{1,0:T(8,128)(2,1)} %bitcast.5, bf16[1792,256]{1,0:T(8,128)(2,1)} %bitcast.6, f32[1,4096]{1,0:T(1,128)} %lgain.1, f32[1,4096]{1,0:T(1,128)} %bitcast.7, bf16[4096,4096]{1,0:T(8,128)(2,1)} %unemb.1, s32[4,64]{1,0:T(4,128)} %ids.1, ...), custom_call_target="tpu_custom_call" | custom-call | tf_op jit(solution)/shard_map/relay/pallas_call | solution.py:712
  155.2 1.3 unpack.1

commit v4 on v3

--- a/solution.py
+++ b/solution.py
@@ -18,11 +18,11 @@
 AHEAD = 2
 END = ((2, 3, 4, 6), (1, 2, 3, 4))
 LAGS = ((2, 4, 6, 7, 8), (2, 4, 5, 6, 7), (2, 3, 4, 5, 6), (1, 2, 3, 4, 5))
-ORDER = (8, 8.1, 8.3, 8.2)
+ORDER = (8, 8.1, 7.9, 7.5)
 WF_SLOT = (-1, 0, 2, 4, 6, 8, 10, 12)
 GATE = 0
 PRE = 4
-CHUNKS = ((0, 256), (256, 512), (768, 512), (1280, 512))
+CHUNKS = ((0, 384), (384, 512), (896, 512), (1408, 384))
 LAG = 2
 NC = len(CHUNKS)
 UROWS = 1024
@@ -571,11 +571,12 @@
         last[h] = slot
     for h in range(NH):
         slot = last[h]
-        at_core(first, slot + 1, 8, y_mid, h, 0)
-        at_core(first, slot + 2, 8, y_end, h, 0)
+        at_core(first, slot + 1, 2.5, y_mid, h, 0)
+        at_core(first, slot + 2, 2.5, y_end, h, 0)
         fns = (y_mid, y_end, finals_one, finals_two, finals_three)
         for lag, fn in zip(LAGS[h], fns):
-            at_core(second, slot + lag, ORDER[h], fn, h, 0)
+            early = h == NH - 2 and fn is y_mid
+            at_core(second, slot + lag, 5.5 if early else ORDER[h], fn, h, 0)
         if h < NH - 1:
             at(slot + LAGS[h][-1], 13, final_norm, h, second)
     end = max(slots) + 1

time: 157 us -> 154 us (0.981)
  Pallas kernels: 156 us -> 153 us
    pallas_call x1, Pallas kernels: 155 us -> 152 us  [run(): pl.pallas_call(body, out_shape=jax.ShapeDtypeStruct((8, 128), f32), in_sp...]
where the time goes in v4:
time: 154 us
  Pallas kernels  153 us (99%)
    pallas_call x1, Pallas kernels, run(): pl.pallas_call(body, out_shape=jax.ShapeDtypeStruct((8, 128), f32), in_sp...  152 us

profile of v4, /device:TPU:1, one launch (start us, length us, event | category | flops | bytes accessed | tf_op | source)
XLA Modules:
  0.0 153.6 jit_solution(4358087481555720670)
XLA Ops:
  0.6 151.5 %relay.1.rows = f32[8,128]{1,0:T(8,128)} custom-call(bf16[4,4,16,4096]{3,2,1,0:T(8,128)(2,1)} %bitcast.4, bf16[256,1792]{1,0:T(8,128)(2,1)} %bitcast.5, bf16[1792,256]{1,0:T(8,128)(2,1)} %bitcast.6, f32[1,4096]{1,0:T(1,128)} %lgain.1, f32[1,4096]{1,0:T(1,128)} %bitcast.7, bf16[4096,4096]{1,0:T(8,128)(2,1)} %unemb.1, s32[4,64]{1,0:T(4,128)} %ids.1, ...), custom_call_target="tpu_custom_call" | custom-call | tf_op jit(solution)/shard_map/relay/pallas_call | solution.py:713
  152.2 1.3 unpack.1

commit v5 on v4

--- a/solution.py
+++ b/solution.py
@@ -501,6 +501,21 @@
             work()
         else:
             pl.when(cond)(work)
+
+    def sent_before(count):
+        batch = pending[:count]
+        del pending[:count]
+        for src, ssem, cond in batch:
+            if cond is None:
+                ref = src() if callable(src) else src
+                pltpu.make_async_copy(ref, ref, sem(ssem)).wait()
+        for which in (first, second):
+            @pl.when(which)
+            def _():
+                for src, ssem, cond in batch:
+                    if cond is which:
+                        ref = src() if callable(src) else src
+                        pltpu.make_async_copy(ref, ref, sem(ssem)).wait()
 
     steps = [(h, c) for c in range(NC) for h in range(2)]
     steps += [(h, c) for h in range(2, NH) for c in range(NC)]
@@ -579,6 +594,11 @@
             at_core(second, slot + lag, 5.5 if early else ORDER[h], fn, h, 0)
         if h < NH - 1:
             at(slot + LAGS[h][-1], 13, final_norm, h, second)
+    share = []
+
+    def old_sends():
+        sent_before(share[0])
+
     end = max(slots) + 1
     for h in range(NH):
         at(end, h, finals_here, h)
@@ -586,7 +606,12 @@
             at(end, h, final_norm, h, first)
         else:
             at(end, h, final_norm, h, None)
+    tail = last[NH - 1]
+    for slot in range(tail + 1, tail + 5):
+        at(slot, 7.4, old_sends)
     for slot in sorted(slots):
+        if slot == tail:
+            share.append(len(pending) // 4)
         for _, _, fn, args, core in sorted(slots[slot], key=lambda e: e[:2]):
             with jax.named_scope(getattr(fn, "__name__", "copy")):
                 if core is None:
@@ -692,17 +717,7 @@
     out[0:4, :] = jnp.concatenate([tok, extra], axis=1)
     out[4:8, :] = jnp.zeros((4, 128), f32)
 
-    for src, ssem, cond in pending:
-        if cond is None:
-            ref = src() if callable(src) else src
-            pltpu.make_async_copy(ref, ref, sem(ssem)).wait()
-    for which in (first, second):
-        @pl.when(which)
-        def _():
-            for src, ssem, cond in pending:
-                if cond is which:
-                    ref = src()
-                    pltpu.make_async_copy(ref, ref, sem(ssem)).wait()
+    sent_before(len(pending))
 
 
 def run(hs, up, down, lgain, fgain, unemb, ids, mask, anchor, pairing):

time: 154 us -> 153 us (level)
  no operation moved by 1% of the time
where the time goes in v5:
time: 153 us
  Pallas kernels  152 us (99%)
    pallas_call x1, Pallas kernels, run(): pl.pallas_call(body, out_shape=jax.ShapeDtypeStruct((8, 128), f32), in_sp...  151 us

profile of v5, /device:TPU:1, one launch (start us, length us, event | category | flops | bytes accessed | tf_op | source)
XLA Modules:
  0.0 153.2 jit_solution(8282211899932572469)
XLA Ops:
  0.6 151.0 %relay.1.rows = f32[8,128]{1,0:T(8,128)} custom-call(bf16[4,4,16,4096]{3,2,1,0:T(8,128)(2,1)} %bitcast.4, bf16[256,1792]{1,0:T(8,128)(2,1)} %bitcast.5, bf16[1792,256]{1,0:T(8,128)(2,1)} %bitcast.6, f32[1,4096]{1,0:T(1,128)} %lgain.1, f32[1,4096]{1,0:T(1,128)} %bitcast.7, bf16[4096,4096]{1,0:T(8,128)(2,1)} %unemb.1, s32[4,64]{1,0:T(4,128)} %ids.1, ...), custom_call_target="tpu_custom_call" | custom-call | tf_op jit(solution)/shard_map/relay/pallas_call | solution.py:728
  151.7 1.3 unpack.1

commit v6 on v5

--- a/solution.py
+++ b/solution.py
@@ -32,7 +32,7 @@
 NS = 1
 SUB = TILE_D // NS
 XB = 4 // NS
-NSEM = 1200
+NSEM = 814
 
 f32 = jnp.float32
 bf16 = jnp.bfloat16

time: 153 us -> 150 us (0.980)
  Pallas kernels: 152 us -> 149 us
    pallas_call x1, Pallas kernels: 151 us -> 148 us  [run(): pl.pallas_call(body, out_shape=jax.ShapeDtypeStruct((8, 128), f32), in_sp...]
where the time goes in v6:
time: 150 us
  Pallas kernels  149 us (99%)
    pallas_call x1, Pallas kernels, run(): pl.pallas_call(body, out_shape=jax.ShapeDtypeStruct((8, 128), f32), in_sp...  148 us

profile of v6, /device:TPU:1, one launch (start us, length us, event | category | flops | bytes accessed | tf_op | source)
XLA Modules:
  0.0 149.7 jit_solution(4098645674736425433)
XLA Ops:
  0.6 147.6 %relay.1.rows = f32[8,128]{1,0:T(8,128)} custom-call(bf16[4,4,16,4096]{3,2,1,0:T(8,128)(2,1)} %bitcast.4, bf16[256,1792]{1,0:T(8,128)(2,1)} %bitcast.5, bf16[1792,256]{1,0:T(8,128)(2,1)} %bitcast.6, f32[1,4096]{1,0:T(1,128)} %lgain.1, f32[1,4096]{1,0:T(1,128)} %bitcast.7, bf16[4096,4096]{1,0:T(8,128)(2,1)} %unemb.1, s32[4,64]{1,0:T(4,128)} %ids.1, ...), custom_call_target="tpu_custom_call" | custom-call | tf_op jit(solution)/shard_map/relay/pallas_call | solution.py:728
  148.2 1.3 unpack.1
